TPU v7x, 32 devices: a whole 2x2x4 slice. The times are simulated.
32 devices in a mesh: row: 2 (over x), col: 4 (over z), chan: 4 (over y, core).
Axes of the slice: x: 2, y: 2, z: 4, core: 2. Of those that a mesh axis runs over, the one named last changes fastest.
Arguments:
- image_gen: float32 [3, 512, 4096], P(None, ('row', 'chan'), 'col'), may hold values from -3 to 3
- image_ref: float32 [3, 512, 4096], P(None, ('row', 'chan'), 'col'), may hold values from -1 to 1
- kernel_one: bfloat16 [3, 3, 48, 64], replicated, may hold values from -0.3125 to 0.3125
- bias_one: float32 [64], replicated, may hold values from -1.5 to 1.5
- kernel_two: bfloat16 [5, 5, 64, 192], replicated, may hold values from -0.15625 to 0.15625
- bias_two: float32 [192], replicated, may hold values from -1.5 to 1.5
- kernel_three: bfloat16 [3, 3, 192, 384], P(None, None, None, 'chan'), may hold values from -0.15625 to 0.15625
- bias_three: float32 [384], replicated, may hold values from -1.5 to 1.5
- lin_first: float32 [64], replicated, may hold values from 0.1 to 1
- lin_second: float32 [192], replicated, may hold values from 0.1 to 1
- lin_third: float32 [384], replicated, may hold values from 0.1 to 1
Outputs:
- image_grad: float32 [3, 512, 4096], P(None, ('row', 'chan'), 'col')
- loss: float32 [], replicated
All inputs are finite; a program needn't handle non-finite values.
Results may differ from a plain program's by a relative error of at most 0.0086.
Values may be sent and summed in bfloat16 or wider, within the bound.
No kernel may reach another device: no remote copies, remote signals or barrier semaphores. Data moves between devices by JAX's collectives and lax.ppermute only.
A program may use at most 128 MiB of HBM per device.

v0:
```python
import functools

import jax
import jax.numpy as jnp
import numpy as np
from jax import lax
from jax.experimental import pallas as pl
from jax.experimental.pallas import tpu as pltpu
from jax.sharding import PartitionSpec as P

OFFSETS = (-0.03, -0.088, -0.188)
SPREADS = (0.458, 0.448, 0.45)
EPSILON = 1e-06

S = 16
HJ = 6
RIM = 12
F32 = jnp.float32
BF16 = jnp.bfloat16
ROWS = ("row", "chan")
GUARD = 128


def up128(n):
    return -(-n // 128) * 128


def wide(column, lanes):
    return jnp.concatenate([column] * (lanes // 128), axis=1)


def column(row, times=1):
    n = row.shape[1]
    here = lax.broadcasted_iota(jnp.int32, (n, n), 0) == lax.broadcasted_iota(jnp.int32, (n, n), 1)
    one = jnp.sum(jnp.where(here, jnp.broadcast_to(row[...], (n, n)), 0.0), axis=1, keepdims=True)
    one = jnp.broadcast_to(one, (n, 128))
    return jnp.concatenate([one] * times, axis=0) if times > 1 else one


def sigmoid(v):
    return 0.5 + 0.5 * jnp.tanh(0.5 * v)


def lanes_of(values, start, count, total):
    part = values[:, start : start + count]
    if total == count:
        return part
    return jnp.concatenate([part, jnp.zeros((values.shape[0], total - count), values.dtype)], axis=1)


def layer_terms(v0, v1, lin, factor):
    g0 = sigmoid(v0)
    f0 = v0 * g0
    f1 = v1 * sigmoid(v1)
    s0 = lax.rsqrt(jnp.sum(f0 * f0, axis=0, keepdims=True) + EPSILON)
    s1 = lax.rsqrt(jnp.sum(f1 * f1, axis=0, keepdims=True) + EPSILON)
    diff = f0 * s0 - f1 * s1
    weighted = lin * diff
    slope = (2.0 * factor) * weighted
    inner = jnp.sum(f0 * slope, axis=0, keepdims=True)
    dfeat = s0 * slope - f0 * (s0 * s0 * s0 * inner)
    return dfeat, g0 * (1.0 + v0 * (1.0 - g0)), jnp.sum(weighted * diff, axis=0, keepdims=True)


def shift_rows(dst, dst_row, dst_lane, src, src_row, count, start, width, chunk=64):
    def body(i, carry):
        a = pl.multiple_of(src_row + i * chunk, chunk)
        b = pl.multiple_of(dst_row + i * chunk, 16)
        part = src[pl.ds(a, chunk), :]
        dst[pl.ds(b, chunk), dst_lane : dst_lane + width] = part[:, start : start + width].astype(BF16)
        return carry

    lax.fori_loop(0, count // chunk, body, 0)


def weights_kernel(R, C, high, across, place, want, k1, k2, k3, w1, w1b, w2, w2b, k3t, masks, t1):
    taps = k1.shape[0]
    ch1 = k1.shape[1]
    pick = lax.broadcasted_iota(jnp.int32, (768, taps), 0) == want[...]
    t1[200:968, :] = jnp.dot(jnp.where(pick, 1.0, 0.0).astype(BF16), k1[...], preferred_element_type=F32)
    t1[0:200, :] = jnp.zeros((200, ch1), F32)
    t1[968:, :] = jnp.zeros((t1.shape[0] - 968, ch1), F32)
    for ci in range(2):
        for cj in range(2):
            moved = t1[200 - cj * 192 - ci * 4 : 968 - cj * 192 - ci * 4, :]
            row = (ci * 2 + cj) * ch1
            w1[row : row + ch1, :] = moved.T.astype(BF16)
    for wi in range(4):
        low = 200 - 4 * (wi % 2)
        half = 1 if wi < 2 else 0
        for wj in range(0, 4, 2):
            parts = []
            for e in range(2):
                start = low + (2 - wj - e) * 192
                block = t1[start : start + 384, :].reshape(24, 2, 8, ch1)[:, half]
                parts.append(block.reshape(192, ch1))
            lane = (wi * 4 + wj) * ch1
            w1b[:, lane : lane + 2 * ch1] = jnp.concatenate(parts, axis=1).astype(BF16)
    size = 5
    ch2 = k2.shape[3]
    none = jnp.zeros((ch1, ch2), F32)

    def tap(y, x):
        return k2[y, x].astype(F32) if 0 <= x < size else none

    for pi in range(2):
        w = 5 * (1 - pi)
        lane = (w // 2) * 12 + (w % 2) * 2
        for x in range(3):
            a = (lane + 4 * x) * ch1
            w2[pi * 2 * ch2 : (pi + 1) * 2 * ch2, a : a + 2 * ch1] = jnp.zeros((2 * ch2, 2 * ch1), BF16)
            a = (lane + 4 * x) * ch2
            w2b[pi * 2 * ch1 : (pi + 1) * 2 * ch1, a : a + 2 * ch2] = jnp.zeros((2 * ch1, 2 * ch2), BF16)
    for y in range(size):
        for pj in range(2):
            for x in range(3):
                pair = jnp.concatenate([tap(y, 2 * x - pj), tap(y, 2 * x + 1 - pj)], axis=0).T.astype(BF16)
                back = jnp.concatenate(
                    [tap(size - 1 - y, size - 1 - 2 * x + pj), tap(size - 1 - y, size - 2 - 2 * x + pj)], axis=1
                ).astype(BF16)
                for pi in range(2):
                    w = y + pi
                    lane = ((w // 2) * 3 + x) * 4 + (w % 2) * 2
                    row = (pi * 2 + pj) * ch2
                    w2[row : row + ch2, lane * ch1 : (lane + 2) * ch1] = pair
                    row = (pi * 2 + pj) * ch1
                    w2b[row : row + ch1, lane * ch2 : (lane + 2) * ch2] = back
    for k in range(0, 9, 2):
        n = min(2, 9 - k) * ch2
        k3t[:, k * ch2 : k * ch2 + n] = k3[k * ch2 : k * ch2 + n, :].astype(F32).T.astype(BF16)
    W = C + 2 * HJ
    lane = lax.broadcasted_iota(jnp.int32, (1, masks.shape[1]), 1)
    i = ((lane.astype(F32) + 0.5) * (1.0 / W)).astype(jnp.int32)
    j = lane - i * W - HJ
    frames = (
        (0, R, False), (0, R + 1, True), (-1, R + 1, True), (-3, R + 6, False), (-2, R + 4, False),
        (-1, R + 2, False), (-1, R + 2, True), (0, R, True), (0, R + 1, False), (-1, R + 1, False),
    )
    masks[...] = jnp.zeros(masks.shape, F32)
    for n, (start, count, mine) in enumerate(frames):
        r, c = i + start, j
        rows, columns = R, C
        if not mine:
            r, c = r + place[0] * R, c + place[1] * C
            rows, columns = R * high, C * across
        ok = (i < count) & (r >= 0) & (r < rows) & (c >= 0) & (c < columns)
        masks[n : n + 1, :] = jnp.where(ok, 1.0, 0.0)


def cells_kernel(R, C, par, img, w1, b1, masks, pre, pool, msg_a, msg_b, sel, z, p1):
    W = C + 2 * HJ
    G = W + 4
    frame = up128((R + 1) * W)
    px = W * S
    K = sel.shape[0]
    rows = R * S + 2 * RIM
    tile = 256
    for t in range(K // tile):
        p = lax.broadcasted_iota(jnp.int32, (K, tile), 0)
        n = lax.broadcasted_iota(jnp.int32, (K, tile), 1) + t * tile
        want = (p & (S - 1)) * G + (p >> 4)
        sel[:, t * tile : (t + 1) * tile] = jnp.where((n == want) & (p < px), 1.0, 0.0).astype(BF16)
    for f in range(2):
        for t in range(K // tile):
            z[f, :, t * tile : (t + 1) * tile] = jnp.dot(
                img[f], sel[:, t * tile : (t + 1) * tile], preferred_element_type=F32
            )
    own = masks[0:1, 0 : R * W]
    bias = wide(column(b1, 4), tile)
    for pi in range(2):
        top = 8 - 8 * pi
        for pj in range(2):
            for f in range(2):
                for s in range(S):
                    q = s + 8 * pj - 4
                    lane = (q % S) * G + q // S
                    parts = []
                    for k in range(R + 1):
                        r = top + S * k
                        parts.append(
                            jnp.concatenate(
                                [z[f, c * rows + r : c * rows + r + S, lane : lane + W] for c in range(3)], axis=0
                            )
                        )
                    parts.append(jnp.zeros((3 * S, frame - (R + 1) * W), F32))
                    p1[s * 48 : s * 48 + 48, f * frame : (f + 1) * frame] = jnp.concatenate(parts, axis=1).astype(BF16)
            for t in range(2 * frame // tile):
                lanes = slice(t * tile, (t + 1) * tile)
                pre[pi, pj, :, lanes] = jnp.dot(w1[...], p1[:, lanes], preferred_element_type=F32) + bias
            for f in range(2):
                v = pre[pi, pj, :, f * frame : (f + 1) * frame]
                feat = v * sigmoid(v)
                quarter = feat.shape[0] // 4
                mean = 0.25 * (
                    (feat[0:quarter] + feat[quarter : 2 * quarter])
                    + (feat[2 * quarter : 3 * quarter] + feat[3 * quarter :])
                )
                mine = mean[:, pi * W : pi * W + R * W]
                mine = jnp.where(own > 0.0, mine, 0.0)
                row = (f * 4 + pi * 2 + pj) * quarter
                even = lax.rem(par[0], 2) == 0
                head = lanes_of(mine, 0, 3 * W, msg_a.shape[1])
                tail = lanes_of(mine, (R - 3) * W, 3 * W, msg_a.shape[1])
                msg_a[row : row + quarter, :] = jnp.where(even, tail, head).astype(BF16)
                msg_b[row : row + quarter, :] = jnp.where(even, head, tail).astype(BF16)
                pool[row : row + quarter, :] = lanes_of(mine, 0, R * W, pool.shape[1]).astype(BF16)


def first_grad_kernel(R, C, pre, lin, masks, w3, base, gain, loss, w3b):
    frame = base.shape[3]
    ch = lin.shape[1]
    c3 = w3.shape[0]
    c2 = w3b.shape[0]
    for k in range(9):
        w3b[:, k * c3 : (k + 1) * c3] = w3[:, (8 - k) * c2 : (9 - k) * c2].astype(F32).T.astype(BF16)
    total = jnp.zeros((1, frame), F32)
    weights = wide(column(lin), frame)
    for pi in range(2):
        for pj in range(2):
            for t in range(4):
                v0 = pre[pi, pj, t * ch : (t + 1) * ch, 0:frame]
                v1 = pre[pi, pj, t * ch : (t + 1) * ch, frame : 2 * frame]
                dfeat, slope, part = layer_terms(v0, v1, weights, 16.0)
                base[pi, pj, t * ch : (t + 1) * ch, :] = dfeat * slope
                gain[pi, pj, t * ch : (t + 1) * ch, :] = 0.25 * slope
                total = total + jnp.where(masks[1 + pi : 2 + pi, 0:frame] > 0.0, part, 0.0)
    loss[...] = jnp.broadcast_to(total, loss.shape)


def middle_kernel(
    R, C, par, pool, rec_a, rec_b, masks, w2, b2, lin2, w3, b3, lin3, w3b, d2, msg_a, msg_b, loss2, loss3,
    s1, p2, pre2, q2, s2, p3, pre3, s3, p3b,
):
    W = C + 2 * HJ
    even = lax.rem(par[0], 2) == 0
    n2 = up128((R + 4) * W)
    n3 = up128((R + 2) * W)
    n4 = up128(R * W)
    c1 = pool.shape[0] // 2
    c2 = b2.shape[1]
    c3 = b3.shape[1]
    ext = s1.shape[1]
    inside = masks[3:4, 0 : (R + 6) * W]
    for r in range(0, 2 * c1, 64):
        a = rec_a[r : r + 64, :].astype(F32)
        b = rec_b[r : r + 64, :].astype(F32)
        above = jnp.where(even, b, a)[:, 0 : 3 * W]
        below = jnp.where(even, a, b)[:, 0 : 3 * W]
        mine = pool[r : r + 64, :].astype(F32)[:, 0 : R * W]
        whole = jnp.concatenate([above, mine, below], axis=1)
        whole = jnp.where(inside > 0.0, whole, 0.0)
        s1[r : r + 64, :] = jnp.concatenate(
            [jnp.zeros((64, GUARD), F32), whole, jnp.zeros((64, ext - GUARD - (R + 6) * W), F32)], axis=1
        )
    for k in range(9):
        off = GUARD + (k // 3) * W + k % 3 - 1
        for f in range(2):
            shift_rows(p2, k * c1, f * n2, s1, f * c1, c1, off, n2)
    tile = 256
    bias2 = column(b2, 4)
    bias3 = column(b3)
    lins3 = column(lin3)

    def second(t, carry):
        lanes = pl.ds(pl.multiple_of(t * tile, tile), tile)
        v = jnp.dot(w2[...], p2[:, lanes], preferred_element_type=F32) + wide(bias2, tile)
        pre2[:, lanes] = v
        feat = v * sigmoid(v)
        q2[:, lanes] = 0.25 * (
            (feat[0:c2] + feat[c2 : 2 * c2]) + (feat[2 * c2 : 3 * c2] + feat[3 * c2 :])
        )
        return carry

    lax.fori_loop(0, 2 * n2 // tile, second, 0)
    for f in range(2):
        good = jnp.where(masks[4:5, 0:n2] > 0.0, q2[:, f * n2 : (f + 1) * n2], 0.0)
        s2[f * c2 : (f + 1) * c2, 0:GUARD] = jnp.zeros((c2, GUARD), F32)
        s2[f * c2 : (f + 1) * c2, GUARD : GUARD + n2] = good
        s2[f * c2 : (f + 1) * c2, GUARD + n2 :] = jnp.zeros((c2, s2.shape[1] - GUARD - n2), F32)
    for k in range(9):
        off = GUARD + (k // 3) * W + k % 3 - 1
        for f in range(2):
            shift_rows(p3, k * c2, f * n3, s2, f * c2, c2, off, n3)

    def third(t, carry):
        lanes = pl.ds(pl.multiple_of(t * tile, tile), tile)
        pre3[:, lanes] = jnp.dot(w3[...], p3[:, lanes], preferred_element_type=F32) + wide(bias3, tile)
        return carry

    lax.fori_loop(0, 2 * n3 // tile, third, 0)
    s3[:, 0:GUARD] = jnp.zeros((c3, GUARD), F32)
    s3[:, GUARD + n3 :] = jnp.zeros((c3, s3.shape[1] - GUARD - n3), F32)
    total = jnp.zeros((1, 128), F32)
    for t in range(n3 // 128):
        v0 = pre3[:, t * 128 : (t + 1) * 128]
        v1 = pre3[:, n3 + t * 128 : n3 + (t + 1) * 128]
        dfeat, slope, part = layer_terms(v0, v1, lins3, 256.0)
        lanes = slice(t * 128, (t + 1) * 128)
        s3[:, GUARD + t * 128 : GUARD + (t + 1) * 128] = jnp.where(masks[5:6, lanes] > 0.0, dfeat * slope, 0.0)
        total = total + jnp.where(masks[6:7, lanes] > 0.0, part, 0.0)
    loss3[...] = jnp.broadcast_to(total, loss3.shape)
    for k in range(9):
        off = GUARD + (k // 3) * W + k % 3 - 1
        shift_rows(p3b, k * c3, 0, s3, 0, c3, off, n4)
    up = 0.25 * jnp.dot(w3b[...], p3b[...], preferred_element_type=F32)
    total2 = jnp.zeros((1, n4), F32)
    weights = wide(column(lin2), n4)
    for t in range(4):
        rows = slice(t * c2, (t + 1) * c2)
        v0 = pre2[rows, 0:n2][:, 2 * W : 2 * W + n4]
        v1 = pre2[rows, n2 : 2 * n2][:, 2 * W : 2 * W + n4]
        dfeat, slope, part = layer_terms(v0, v1, weights, 64.0)
        d = jnp.where(masks[0:1, 0:n4] > 0.0, (dfeat + up) * slope, 0.0)
        d2[rows, :] = d.astype(BF16)
        total2 = total2 + jnp.where(masks[7:8, 0:n4] > 0.0, part, 0.0)
        head = lanes_of(d, 0, 2 * W, msg_a.shape[1])
        tail = lanes_of(d, (R - 2) * W, 2 * W, msg_a.shape[1])
        msg_a[rows, :] = jnp.where(even, tail, head).astype(BF16)
        msg_b[rows, :] = jnp.where(even, head, tail).astype(BF16)
    loss2[...] = jnp.broadcast_to(total2, loss2.shape)


def last_kernel(
    R, C, par, d2, rec_a, rec_b, masks, w2b, base, gain, w1b, out, s4, p2b, s5, p1b, g, sel, flat
):
    W = C + 2 * HJ
    even = lax.rem(par[0], 2) == 0
    c2 = d2.shape[0]
    frame = base.shape[3]
    n4 = up128(R * W)
    ext = s4.shape[1]
    ch = w2b.shape[0] // 4
    inside = masks[4:5, 0 : (R + 4) * W]

    def join(i, carry):
        rows = pl.ds(pl.multiple_of(i * 64, 64), 64)
        a = rec_a[rows, :].astype(F32)
        b = rec_b[rows, :].astype(F32)
        above = jnp.where(even, b, a)[:, 0 : 2 * W]
        below = jnp.where(even, a, b)[:, 0 : 2 * W]
        mine = d2[rows, :].astype(F32)[:, 0 : R * W]
        whole = jnp.concatenate([above, mine, below], axis=1)
        whole = jnp.where(inside > 0.0, whole, 0.0)
        s4[rows, :] = jnp.concatenate(
            [jnp.zeros((64, GUARD), F32), whole, jnp.zeros((64, ext - GUARD - (R + 4) * W), F32)], axis=1
        )
        return carry

    lax.fori_loop(0, c2 // 64, join, 0)
    for qi in range(2):
        for k in range(9):
            off = GUARD + (k // 3 + 1 - qi) * W + k % 3 - 1
            shift_rows(p2b, k * c2, 0, s4, 0, c2, off, frame)
        up = jnp.dot(w2b[qi * 2 * ch : (qi + 1) * 2 * ch, :], p2b[...], preferred_element_type=F32)
        good = masks[8 + qi : 9 + qi, 0:frame] > 0.0
        for qj in range(2):
            part = up[qj * ch : (qj + 1) * ch]
            for t in range(4):
                rows = slice(t * ch, (t + 1) * ch)
                d = base[qi, qj, rows, :] + gain[qi, qj, rows, :] * part
                row = ((qi * 2 + qj) * 4 + t) * ch
                s5[row : row + ch, 0:GUARD] = jnp.zeros((ch, GUARD), F32)
                s5[row : row + ch, GUARD : GUARD + frame] = jnp.where(good, d, 0.0)
                s5[row : row + ch, GUARD + frame :] = jnp.zeros((ch, s5.shape[1] - GUARD - frame), F32)
    for qi in range(2):
        for qj in range(2):
            for wi in range(4):
                for wj in range(4):
                    y, x = 2 * qi + wi - 1, 2 * qj + wj - 1
                    dy, dx = y // 4, x // 4
                    y, x = y % 4, x % 4
                    row = (((y // 2) * 2 + x // 2) * 4 + (y % 2) * 2 + x % 2) * ch
                    off = GUARD + (dy + y // 2) * W + dx
                    p1b[(wi * 4 + wj) * ch : (wi * 4 + wj + 1) * ch, :] = s5[row : row + ch, :][
                        :, off : off + n4
                    ].astype(BF16)
            g[qi, qj] = jnp.dot(w1b[...], p1b[...], preferred_element_type=F32)
    for s in range(0, S, 2):
        for c in range(3):
            for i in range(R):
                for qi in range(2):
                    parts = []
                    for e in range(2):
                        q = s + e
                        r = ((q % 8) * 3 + c) * 8
                        lane = i * W + HJ
                        parts.append(g[qi, q // 8, r : r + 8, lane : lane + C])
                    row = c * R * S + i * S + qi * 8
                    flat[row : row + 8, s * C : (s + 2) * C] = jnp.concatenate(parts, axis=1)
    K = S * C
    tile = 256
    for t in range(K // tile):
        p = lax.broadcasted_iota(jnp.int32, (tile, K), 0) + t * tile
        n = lax.broadcasted_iota(jnp.int32, (tile, K), 1)
        group = p // C
        sel[t * tile : (t + 1) * tile, :] = jnp.where(n == (p - group * C) * S + group, 1.0, 0.0).astype(BF16)
    v = flat[...]
    high = v.astype(BF16)
    low = (v - high.astype(F32)).astype(BF16)
    flat[...] = jnp.dot(high, sel[...], preferred_element_type=F32) + jnp.dot(
        low, sel[...], preferred_element_type=F32
    )
    for c in range(3):
        out[c] = flat[c * R * S : (c + 1) * R * S, :] / SPREADS[c]


def swap(a, b, axis):
    count = lax.axis_size(axis)
    first = lax.ppermute(a, axis, [(i, i ^ 1) for i in range(count)])
    second = [(i, (i + 1) % count) for i in range(1, count, 2)]
    second = second + [(j, i) for i, j in second]
    return first, lax.ppermute(b, axis, second)


def neighbours(values, dim, width, axis, where, count):
    even = where % 2 == 0
    size = values.shape[dim]
    head = lax.slice_in_dim(values, 0, width, axis=dim)
    tail = lax.slice_in_dim(values, size - width, size, axis=dim)
    a, b = swap(jnp.where(even, tail, head), jnp.where(even, head, tail), axis)
    zero = jnp.zeros_like(head)
    before = jnp.where(where > 0, jnp.where(even, b, a), zero)
    after = jnp.where(where < count - 1, jnp.where(even, a, b), zero)
    return before, after


def call(kernel, outs, scratch, *args):
    specs = [pl.BlockSpec(memory_space=pltpu.SMEM if a.ndim == 1 else pltpu.VMEM) for a in args]
    return pl.pallas_call(
        kernel,
        out_shape=outs,
        in_specs=specs,
        out_specs=jax.tree.map(lambda _: pl.BlockSpec(memory_space=pltpu.VMEM), outs),
        scratch_shapes=scratch,
        compiler_params=pltpu.CompilerParams(vmem_limit_bytes=56 * 2**20),
    )(*args)


def local(
    image_gen, image_ref, kernel_one, bias_one, kernel_two, bias_two, kernel_three, bias_three,
    lin_first, lin_second, lin_third,
):
    R = image_gen.shape[1] // S
    C = image_gen.shape[2] // S
    W = C + 2 * HJ
    high = lax.axis_size("row") * lax.axis_size("chan")
    across = lax.axis_size("col")
    at_row = lax.axis_index("row") * lax.axis_size("chan") + lax.axis_index("chan")
    at_col = lax.axis_index("col")
    pixels = image_gen.shape[1] * image_gen.shape[2] * high * across
    ch1, ch2, ch3 = bias_one.shape[0], bias_two.shape[0], bias_three.shape[0]

    offsets = jnp.array(OFFSETS, F32)[:, None, None]
    spreads = jnp.array(SPREADS, F32)[:, None, None]
    both = jnp.stack([((image - offsets) / spreads).astype(BF16) for image in (image_gen, image_ref)])
    left, right = neighbours(both, 3, HJ * S, "col", at_col, across)
    rim = jnp.concatenate([left, both, right], axis=3)
    over, under = neighbours(rim, 2, RIM, ROWS, at_row, high)
    rim = jnp.concatenate([over, rim, under], axis=2)
    span = (W + 4) * S
    rim = jnp.pad(rim, ((0, 0), (0, 0), (0, 0), (0, span - W * S)))
    rim = rim.reshape(2, 3 * (R * S + 2 * RIM), span)

    y, x, c, a, b = np.meshgrid(*(np.arange(n) for n in (3, 3, 3, 4, 4)), indexing="ij")
    want = jnp.asarray((x * 192 + b * 48 + c * 16 + y * 4 + a).reshape(1, -1), jnp.int32)
    place = jnp.stack([at_row, at_col]).astype(jnp.int32)
    shard = kernel_three.shape[3]

    def arr(shape, dtype=F32):
        return jax.ShapeDtypeStruct(shape, dtype)

    w1, w1b, w2, w2b, mine, masks = call(
        functools.partial(weights_kernel, R, C, high, across),
        (
            arr((4 * ch1, 768), BF16),
            arr((192, 16 * ch1), BF16),
            arr((4 * ch2, 36 * ch1), BF16),
            arr((4 * ch1, 36 * ch2), BF16),
            arr((shard, 9 * ch2), BF16),
            arr((16, 1024)),
        ),
        [pltpu.VMEM((976, ch1), F32)],
        place, want, kernel_one.reshape(-1, ch1), kernel_two, kernel_three.reshape(-1, shard),
    )
    parts = lax.axis_size("chan")
    whole = mine[None]
    step = 1
    here = lax.axis_index("chan")
    while step < parts:
        other = lax.ppermute(whole, "chan", [(i, i ^ step) for i in range(parts)])
        first = (here & step) == 0
        whole = jnp.concatenate([jnp.where(first, whole, other), jnp.where(first, other, whole)])
        step *= 2
    w3 = whole.reshape(ch3, 9 * ch2)

    def flat(values):
        return values.reshape(1, -1)

    b1, b2, b3 = flat(bias_one), flat(bias_two), flat(bias_three)
    lin1, lin2, lin3 = flat(lin_first), flat(lin_second), flat(lin_third)

    frame = up128((R + 1) * W)
    n2, n3, n4 = up128((R + 4) * W), up128((R + 2) * W), up128(R * W)
    rows = 3 * (R * S + 2 * RIM)

    pre, pool, msg_a, msg_b = call(
        functools.partial(cells_kernel, R, C),
        (
            arr((2, 2, 4 * ch1, 2 * frame)),
            arr((8 * ch1, n4), BF16),
            arr((8 * ch1, up128(3 * W)), BF16),
            arr((8 * ch1, up128(3 * W)), BF16),
        ),
        [pltpu.VMEM((span, span), BF16), pltpu.VMEM((2, rows, span), F32), pltpu.VMEM((768, 2 * frame), BF16)],
        place, rim, w1, b1, masks,
    )
    rec_a, rec_b = swap(msg_a, msg_b, ROWS)
    base, gain, loss1, w3b = call(
        functools.partial(first_grad_kernel, R, C),
        (arr((2, 2, 4 * ch1, frame)), arr((2, 2, 4 * ch1, frame)), arr((8, frame)), arr((ch2, 9 * ch3), BF16)),
        [],
        pre, lin1, masks, w3,
    )
    ext1 = GUARD + up128((R + 6) * W) + GUARD
    d2, msg_a, msg_b, loss2, loss3 = call(
        functools.partial(middle_kernel, R, C),
        (
            arr((4 * ch2, n4), BF16),
            arr((4 * ch2, up128(2 * W)), BF16),
            arr((4 * ch2, up128(2 * W)), BF16),
            arr((8, n4)),
            arr((8, 128)),
        ),
        [
            pltpu.VMEM((8 * ch1, ext1), F32),
            pltpu.VMEM((36 * ch1, 2 * n2), BF16),
            pltpu.VMEM((4 * ch2, 2 * n2), F32),
            pltpu.VMEM((ch2, 2 * n2), F32),
            pltpu.VMEM((2 * ch2, GUARD + n2 + GUARD), F32),
            pltpu.VMEM((9 * ch2, 2 * n3), BF16),
            pltpu.VMEM((ch3, 2 * n3), F32),
            pltpu.VMEM((ch3, GUARD + n3 + GUARD), F32),
            pltpu.VMEM((9 * ch3, n4), BF16),
        ],
        place, pool, rec_a, rec_b, masks, w2, b2, lin2, w3, b3, lin3, w3b,
    )
    rec_a, rec_b = swap(msg_a, msg_b, ROWS)
    partial_loss = (
        jnp.sum(loss1[0]) / (pixels // 16) + jnp.sum(loss2[0]) / (pixels // 64) + jnp.sum(loss3[0]) / (pixels // 256)
    )
    everyone = high * across
    spread_out = jnp.broadcast_to(partial_loss, (everyone, 8, 128))
    loss = jnp.sum(lax.all_to_all(spread_out, ("row", "col", "chan"), 0, 0)[:, 0, 0])
    image_grad = call(
        functools.partial(last_kernel, R, C),
        arr(image_gen.shape),
        [
            pltpu.VMEM((4 * ch2, GUARD + up128((R + 4) * W) + GUARD), F32),
            pltpu.VMEM((36 * ch2, frame), BF16),
            pltpu.VMEM((16 * ch1, GUARD + frame + GUARD), F32),
            pltpu.VMEM((16 * ch1, n4), BF16),
            pltpu.VMEM((2, 2, 192, n4), F32),
            pltpu.VMEM((S * C, S * C), BF16),
            pltpu.VMEM((3 * R * S, S * C), F32),
        ],
        place, d2, rec_a, rec_b, masks, w2b, base, gain, w1b,
    )
    return image_grad, loss


def solution(mesh):
    tile = P(None, ROWS, "col")
    return jax.shard_map(
        local,
        mesh=mesh,
        in_specs=(tile, tile, P(), P(), P(), P(), P(None, None, None, "chan"), P(), P(), P(), P()),
        out_specs=(tile, P()),
        check_vma=False,
    )
```

profile of v0, /device:TPU:0, one launch (start us, length us, event | category | flops | bytes accessed | tf_op | source)
XLA Modules:
  0.0 133.4 jit_solution(11827309950464965656)
XLA Ops:
  0.7 0.6 pad_add_fusion.place.par
  1.3 5.9 %shard_map.149 = (bf16[256,768]{1,0:T(8,128)(2,1)}, bf16[192,1024]{1,0:T(8,128)(2,1)}, bf16[768,2304]{1,0:T(8,128)(2,1)}, bf16[256,6912]{1,0:T(8,128)(2,1)}, bf1...) custom-call(s32[2]{0:T(128)} %pad_add_fusion.place.par, s32[1,432]{1,0:T(1,128)} %constant.61.clone.want, ...), custom_call_target="tpu_custom_call" | custom-call | tf_op jit(solution)/shard_map/pallas_call | solution.py:429
  7.2 0.5 collective-permute-start.6
  7.7 1.4 %fusion.5 = (bf16[1,3,64,1024]{3,2,1,0:T(8,128)(2,1)S(1)}, bf16[1,3,64,1024]{3,2,1,0:T(8,128)(2,1)S(1)}) fusion(f32[3,64,1024]{2,1,0:T(8,128)S(1)} %copy-done, f32[3]{0:T(128)S(1)} %copy-done.8, f32[3]{0:T(128)S(1)} %copy-done.9, f32[3,64,1024]{2,1,0:T(8,128)} %param.15), kind=kLoop, calls=%fused_computation.17 | loop fusion | flops 1179648 | bytes 2359320 | tf_op jit(solution)/shard_map/stack | solution.py:455
  9.2 4.7 %collective-permute-start = (bf16[2,3,64,96]{3,2,1,0:T(8,128)(2,1)S(1)}, bf16[2,3,64,96]{3,2,1,0:T(8,128)(2,1)S(1)}, u32[]{:S(2)}, u32[]{:S(2)}) collective-permute-start(bf16[2,3,64,96]{3,2,1,0:T(8,128)(2,1)S(1)} %broadcast_select_fusion.7), channel_id=1, source_target_pairs={{4,8},{12,0},{8,4},{0,12},{5,9},{13,1},{9,5},{1,13},{6,10},{14,2},... | collective-permute-start | bytes 221192 | tf_op jit(solution)/shard_map/ppermute | solution.py:412
  13.9 0.6 reshape.43.b3
  14.5 0.6 reshape.44.lin3
  15.1 2.4 %collective-permute-done = bf16[2,3,64,96]{3,2,1,0:T(8,128)(2,1)S(1)} collective-permute-done((bf16[2,3,64,96]{3,2,1,0:T(8,128)(2,1)S(1)}, bf16[2,3,64,96]{3,2,1,0:T(8,128)(2,1)S(1)}, u32[]{:S(2)}, u32[]{:S(2)}) %collective-permute-start) | collective-permute-done | bytes 73760 | tf_op jit(solution)/shard_map/ppermute | solution.py:412
  17.6 2.0 %collective-permute-done.1 = bf16[2,3,64,96]{3,2,1,0:T(8,128)(2,1)S(1)} collective-permute-done((bf16[2,3,64,96]{3,2,1,0:T(8,128)(2,1)S(1)}, bf16[2,3,64,96]{3,2,1,0:T(8,128)(2,1)S(1)}, u32[]{:S(2)}, u32[]{:S(2)}) %collective-permute-start.1) | collective-permute-done | bytes 73760 | tf_op jit(solution)/shard_map/ppermute | solution.py:409
  19.6 1.1 concatenate.12
  20.8 2.0 %collective-permute-start.2 = (bf16[2,3,12,1216]{3,2,1,0:T(8,128)(2,1)S(1)}, bf16[2,3,12,1216]{3,2,1,0:T(8,128)(2,1)S(1)}, u32[]{:S(2)}, u32[]{:S(2)}) collective-permute-start(bf16[2,3,12,1216]{3,2,1,0:T(8,128)(2,1)S(1)} %get-tuple-element.45), channel_id=1, source_target_pairs={{1,2},{3,16},{17,18},{19,0},{2,1},{16,3},{18,17},{0,19},{5,6},{7,2... | collective-permute-start | bytes 525320 | tf_op jit(solution)/shard_map/ppermute | solution.py:412
  23.0 1.2 collective-permute-start.7
  24.1 3.4 %collective-permute-done.2 = bf16[2,3,12,1216]{3,2,1,0:T(8,128)(2,1)S(1)} collective-permute-done((bf16[2,3,12,1216]{3,2,1,0:T(8,128)(2,1)S(1)}, bf16[2,3,12,1216]{3,2,1,0:T(8,128)(2,1)S(1)}, u32[]{:S(2)}, u32[]{:S(2)}) %collective-permute-start.2) | collective-permute-done | bytes 175136 | tf_op jit(solution)/shard_map/ppermute | solution.py:412
  27.5 1.5 %fusion.4 = bf16[2,3,88,1280]{3,2,1,0:T(8,128)(2,1)} fusion(bf16[2,3,12,1216]{3,2,1,0:T(8,128)(2,1)S(1)} %get-tuple-element.50, bf16[2,3,64,1216]{3,2,1,0:T(8,128)(2,1)S(1)} %concatenate.12, bf16[2,3,12,1216]{3,2,1,0:T(8,128)(2,1)S(1)} %get-tuple-element.49), kind=kLoop, calls=%fused_computation.6 | loop fusion | flops 6758400 | bytes 2635776 | tf_op jit(solution)/shard_map/concatenate | solution.py:459
  29.0 9.0 %shard_map.150 = (f32[2,2,256,768]{3,2,1,0:T(8,128)}, bf16[512,384]{1,0:T(8,128)(2,1)}, bf16[512,256]{1,0:T(8,128)(2,1)}, bf16[512,256]{1,0:T(8,128)(2,1)}) custom-call(s32[2]{0:T(128)} %pad_add_fusion.place.par, bf16[2,264,1280]{2,1,0:T(8,128)(2,1)} %bitcast.19, bf16[256,768]{1,0:T(8,128)(2,1)} %get-tuple-element.21.w1, f32[1,64]{1,0:T(1,128)} %bitcast.25, ...), custom_call_target="tpu_custom_call" | custom-call | tf_op jit(solution)/shard_map/pallas_call | solution.py:429
  38.0 3.5 %collective-permute-start.4 = (bf16[512,256]{1,0:T(8,128)(2,1)}, bf16[512,256]{1,0:T(8,128)(2,1)S(1)}, u32[]{:S(2)}, u32[]{:S(2)}) collective-permute-start(bf16[512,256]{1,0:T(8,128)(2,1)} %get-tuple-element.24), channel_id=1, source_target_pairs={{0,1},{1,0},{2,3},{3,2},{16,17},{17,16},{18,19},{19,18},{4,5},{5,4... | collective-permute-start | bytes 786440 | tf_op jit(solution)/shard_map/ppermute | solution.py:409
  41.5 2.2 %collective-permute-start.5 = (bf16[512,256]{1,0:T(8,128)(2,1)}, bf16[512,256]{1,0:T(8,128)(2,1)S(1)}, u32[]{:S(2)}, u32[]{:S(2)}) collective-permute-start(bf16[512,256]{1,0:T(8,128)(2,1)} %get-tuple-element.25), channel_id=1, source_target_pairs={{1,2},{3,16},{17,18},{19,0},{2,1},{16,3},{18,17},{0,19},{5,6},{7,2... | collective-permute-start | bytes 786440 | tf_op jit(solution)/shard_map/ppermute | solution.py:412
  43.7 0.4 collective-permute-done.7
  44.2 1.2 pad_maximum_fusion
  45.4 6.6 %shard_map.151 = (f32[2,2,256,384]{3,2,1,0:T(8,128)}, f32[2,2,256,384]{3,2,1,0:T(8,128)}, f32[8,384]{1,0:T(8,128)}, bf16[192,3456]{1,0:T(8,128)(2,1)}) custom-call(f32[2,2,256,768]{3,2,1,0:T(8,128)} %get-tuple-element.28.pre, f32[1,64]{1,0:T(1,128)} %bitcast.26, f32[16,1024]{1,0:T(8,128)} %get-tuple-element.22.masks, bf16[384,1728]{1,0:T(8,128)(2,1)} %bitcast.17), custom_call_target="tpu_custom_call" | custom-call | tf_op jit(solution)/shard_map/pallas_call | solution.py:429
  52.0 0.7 copy-done.4
  52.7 0.1 copy-done.5
  52.8 31.8 %shard_map.152 = (bf16[768,384]{1,0:T(8,128)(2,1)}, bf16[768,256]{1,0:T(8,128)(2,1)}, bf16[768,256]{1,0:T(8,128)(2,1)}, f32[8,384]{1,0:T(8,128)}, f32[8,128]{1,0:T(8,128)}) custom-call(s32[2]{0:T(128)} %pad_add_fusion.place.par, bf16[512,384]{1,0:T(8,128)(2,1)} %get-tuple-element.23.pool, bf16[512,256]{1,0:T(8,128)(2,1)} %copy-done.4, ...), custom_call_target="tpu_custom_call" | custom-call | tf_op jit(solution)/shard_map/pallas_call | solution.py:429
  84.6 1.4 %slice_reduce_fusion.1 = f32[]{:T(128)} fusion(f32[8,384]{1,0:T(8,128)} %get-tuple-element.38), kind=kLoop, calls=%fused_computation.32 | loop fusion | flops 383 | bytes 1540 | tf_op jit(solution)/shard_map/reduce_sum | solution.py:549
  86.0 1.3 slice_reduce_fusion.2
  87.4 1.7 %collective-permute-start.9 = (bf16[768,256]{1,0:T(8,128)(2,1)}, bf16[768,256]{1,0:T(8,128)(2,1)S(1)}, u32[]{:S(2)}, u32[]{:S(2)}) collective-permute-start(bf16[768,256]{1,0:T(8,128)(2,1)} %get-tuple-element.32), channel_id=1, source_target_pairs={{1,2},{3,16},{17,18},{19,0},{2,1},{16,3},{18,17},{0,19},{5,6},{7,2... | collective-permute-start | bytes 1179656 | tf_op jit(solution)/shard_map/ppermute | solution.py:412
  89.0 1.4 %slice_reduce_fusion.3 = f32[]{:T(128)} fusion(f32[8,128]{1,0:T(8,128)} %get-tuple-element.39), kind=kLoop, calls=%fused_computation.35 | loop fusion | flops 127 | bytes 516 | tf_op jit(solution)/shard_map/reduce_sum | solution.py:549
  92.4 11.1 %all_to_all.5 = f32[32,8,128]{2,1,0:T(8,128)S(1)} all-to-all(f32[32,8,128]{2,1,0:T(8,128)S(1)} %broadcast_in_dim.17), channel_id=1, replica_groups=mesh['row'=2,'col'=4,'chan'=4] {'row','col','chan'}, dimensions={0} | all-to-all | bytes 262144 | tf_op jit(solution)/shard_map/all_to_all | solution.py:553
  103.5 0.6 slice_reduce_fusion
  104.2 0.8 copy-done.1
  104.9 0.2 copy-done.2
  105.1 28.3 %shard_map.153 = f32[3,64,1024]{2,1,0:T(8,128)} custom-call(s32[2]{0:T(128)} %pad_add_fusion.place.par, bf16[768,384]{1,0:T(8,128)(2,1)} %get-tuple-element.30.d2, bf16[768,256]{1,0:T(8,128)(2,1)} %copy-done.1, bf16[768,256]{1,0:T(8,128)(2,1)} %copy-done.2, f32[16,1024]{1,0:T(8,128)} %get-tuple-element.22.masks, bf16[256,6912]{1,0:T(8,128)(2,1)} %get-tuple-element.33.w2b, ...), custom_call_target="tpu_custom_call" | custom-call | tf_op jit(solution)/shard_map/pallas_call | solution.py:429
  (35 shorter events, 0.6 us)
Async XLA Ops:
  0.6 7.0 %copy-start.8 = (f32[3]{0:T(128)S(1)}, f32[3]{0:T(128)}, u32[]{:S(2)}) copy-start(f32[3]{0:T(128)} %constant.64) | copy-start | bytes 40
  0.6 7.0 %copy-start.9 = (f32[3]{0:T(128)S(1)}, f32[3]{0:T(128)}, u32[]{:S(2)}) copy-start(f32[3]{0:T(128)} %constant.66) | copy-start | bytes 40
  0.7 7.0 %copy-start = (f32[3,64,1024]{2,1,0:T(8,128)S(1)}, f32[3,64,1024]{2,1,0:T(8,128)}, u32[]{:S(2)}) copy-start(f32[3,64,1024]{2,1,0:T(8,128)} %param.14) | copy-start | bytes 2359300
  7.2 15.7 %collective-permute-start.6 = (bf16[1,96,1728]{2,1,0:T(8,128)(2,1)}, bf16[1,96,1728]{2,1,0:T(8,128)(2,1)S(1)}, u32[]{:S(2)}, u32[]{:S(2)}) collective-permute-start(bf16[1,96,1728]{2,1,0:T(8,128)(2,1)} %bitcast.21), channel_id=1, source_target_pairs={{0,1},{1,0},{2,3},{3,2},{4,5},{5,4},{6,7},{7,6},{8,9},{9,8},{10,11... | collective-permute-start | bytes 995336 | tf_op jit(solution)/shard_map/ppermute | solution.py:490
  7.7 6.2 %copy-start.6 = (f32[384]{0:T(512)S(1)}, f32[384]{0:T(512)}, u32[]{:S(2)}) copy-start(f32[384]{0:T(512)} %param.21) | copy-start | bytes 4612
  7.7 6.8 %copy-start.7 = (f32[384]{0:T(512)S(1)}, f32[384]{0:T(512)}, u32[]{:S(2)}) copy-start(f32[384]{0:T(512)} %param.24) | copy-start | bytes 4612
  9.2 8.4 %collective-permute-start = (bf16[2,3,64,96]{3,2,1,0:T(8,128)(2,1)S(1)}, bf16[2,3,64,96]{3,2,1,0:T(8,128)(2,1)S(1)}, u32[]{:S(2)}, u32[]{:S(2)}) collective-permute-start(bf16[2,3,64,96]{3,2,1,0:T(8,128)(2,1)S(1)} %broadcast_select_fusion.7), channel_id=1, source_target_pairs={{4,8},{12,0},{8,4},{0,12},{5,9},{13,1},{9,5},{1,13},{6,10},{14,2},... | collective-permute-start | bytes 221192 | tf_op jit(solution)/shard_map/ppermute | solution.py:412
  13.9 5.7 %collective-permute-start.1 = (bf16[2,3,64,96]{3,2,1,0:T(8,128)(2,1)S(1)}, bf16[2,3,64,96]{3,2,1,0:T(8,128)(2,1)S(1)}, u32[]{:S(2)}, u32[]{:S(2)}) collective-permute-start(bf16[2,3,64,96]{3,2,1,0:T(8,128)(2,1)S(1)} %get-tuple-element.40), channel_id=1, source_target_pairs={{0,4},{4,0},{8,12},{12,8},{1,5},{5,1},{9,13},{13,9},{2,6},{6,2},{1... | collective-permute-start | bytes 221192 | tf_op jit(solution)/shard_map/ppermute | solution.py:409
  19.5 3.3 %copy-start.3 = (bf16[96,1728]{1,0:T(8,128)(2,1)S(1)}, bf16[96,1728]{1,0:T(8,128)(2,1)}, u32[]{:S(2)}) copy-start(bf16[96,1728]{1,0:T(8,128)(2,1)} %get-tuple-element.27) | copy-start | bytes 995332
  20.8 6.7 %collective-permute-start.2 = (bf16[2,3,12,1216]{3,2,1,0:T(8,128)(2,1)S(1)}, bf16[2,3,12,1216]{3,2,1,0:T(8,128)(2,1)S(1)}, u32[]{:S(2)}, u32[]{:S(2)}) collective-permute-start(bf16[2,3,12,1216]{3,2,1,0:T(8,128)(2,1)S(1)} %get-tuple-element.45), channel_id=1, source_target_pairs={{1,2},{3,16},{17,18},{19,0},{2,1},{16,3},{18,17},{0,19},{5,6},{7,2... | collective-permute-start | bytes 525320 | tf_op jit(solution)/shard_map/ppermute | solution.py:412
  22.8 4.7 %collective-permute-start.3 = (bf16[2,3,12,1216]{3,2,1,0:T(8,128)(2,1)S(1)}, bf16[2,3,12,1216]{3,2,1,0:T(8,128)(2,1)S(1)}, u32[]{:S(2)}, u32[]{:S(2)}) collective-permute-start(bf16[2,3,12,1216]{3,2,1,0:T(8,128)(2,1)S(1)} %get-tuple-element.46), channel_id=1, source_target_pairs={{0,1},{1,0},{2,3},{3,2},{16,17},{17,16},{18,19},{19,18},{4,5},{5,4... | collective-permute-start | bytes 525320 | tf_op jit(solution)/shard_map/ppermute | solution.py:409
  23.0 21.1 %collective-permute-start.7 = (bf16[2,96,1728]{2,1,0:T(8,128)(2,1)S(1)}, bf16[2,96,1728]{2,1,0:T(8,128)(2,1)S(1)}, u32[]{:S(2)}, u32[]{:S(2)}) collective-permute-start(bf16[2,96,1728]{2,1,0:T(8,128)(2,1)S(1)} %pad_maximum_fusion.2), channel_id=1, source_target_pairs={{0,2},{1,3},{2,0},{3,1},{4,6},{5,7},{6,4},{7,5},{8,10},{9,11},{10,... | collective-permute-start | bytes 1990664 | tf_op jit(solution)/shard_map/ppermute | solution.py:490
  38.0 14.0 %collective-permute-start.4 = (bf16[512,256]{1,0:T(8,128)(2,1)}, bf16[512,256]{1,0:T(8,128)(2,1)S(1)}, u32[]{:S(2)}, u32[]{:S(2)}) collective-permute-start(bf16[512,256]{1,0:T(8,128)(2,1)} %get-tuple-element.24), channel_id=1, source_target_pairs={{0,1},{1,0},{2,3},{3,2},{16,17},{17,16},{18,19},{19,18},{4,5},{5,4... | collective-permute-start | bytes 786440 | tf_op jit(solution)/shard_map/ppermute | solution.py:409
  41.5 10.5 %collective-permute-start.5 = (bf16[512,256]{1,0:T(8,128)(2,1)}, bf16[512,256]{1,0:T(8,128)(2,1)S(1)}, u32[]{:S(2)}, u32[]{:S(2)}) collective-permute-start(bf16[512,256]{1,0:T(8,128)(2,1)} %get-tuple-element.25), channel_id=1, source_target_pairs={{1,2},{3,16},{17,18},{19,0},{2,1},{16,3},{18,17},{0,19},{5,6},{7,2... | collective-permute-start | bytes 786440 | tf_op jit(solution)/shard_map/ppermute | solution.py:412
  52.0 0.7 copy-start.4
  52.0 0.8 copy-start.5
  87.4 16.8 %collective-permute-start.8 = (bf16[768,256]{1,0:T(8,128)(2,1)}, bf16[768,256]{1,0:T(8,128)(2,1)S(1)}, u32[]{:S(2)}, u32[]{:S(2)}) collective-permute-start(bf16[768,256]{1,0:T(8,128)(2,1)} %get-tuple-element.31), channel_id=1, source_target_pairs={{0,1},{1,0},{2,3},{3,2},{16,17},{17,16},{18,19},{19,18},{4,5},{5,4... | collective-permute-start | bytes 1179656 | tf_op jit(solution)/shard_map/ppermute | solution.py:409
  87.4 16.8 %collective-permute-start.9 = (bf16[768,256]{1,0:T(8,128)(2,1)}, bf16[768,256]{1,0:T(8,128)(2,1)S(1)}, u32[]{:S(2)}, u32[]{:S(2)}) collective-permute-start(bf16[768,256]{1,0:T(8,128)(2,1)} %get-tuple-element.32), channel_id=1, source_target_pairs={{1,2},{3,16},{17,18},{19,0},{2,1},{16,3},{18,17},{0,19},{5,6},{7,2... | collective-permute-start | bytes 1179656 | tf_op jit(solution)/shard_map/ppermute | solution.py:412
  104.1 0.8 copy-start.1
  104.1 1.0 copy-start.2
where the time goes:
time: 134 us; the launch traced here: 133 us
  Pallas kernels  81.6 us (61%)
  starting transfers between devices  15.7 us (12%)
  blocking collectives  11.1 us (8%)
  other arithmetic  9.9 us (7%)
  waiting for transfers between devices  8.12 us (6%)
  local copies, waits for them, and re-layouts  4.15 us (3%)
  between operations  2.84 us (2%)
    pallas_call x5, Pallas kernels, call(): pl.pallas_call(kernel, out_shape=outs, in_specs=specs, out_specs=jax.tree...  81.6 us
    all_to_all x1, blocking collectives, local(): lax.all_to_all(spread_out, ('row', 'col', 'chan'), 0, 0)[:, 0, 0]  11.1 us
    ppermute x4, starting transfers between devices, swap(): return (first, lax.ppermute(b, axis, second))  10.6 us
    ppermute x4, waiting for transfers between devices, swap(): return (first, lax.ppermute(b, axis, second))  5.79 us
    ppermute x4, starting transfers between devices, swap(): first = lax.ppermute(a, axis, [(i, i ^ 1) for i in range(count)])  3.52 us
  transfers between devices with their start and end apart: 10, of which 4 were waited for; matrix products, arithmetic and copies ran while one was open for 7% of the time, Pallas kernels for 12%

commit v1 on v0

--- a/solution.py
+++ b/solution.py
@@ -62,18 +62,22 @@
     return dfeat, g0 * (1.0 + v0 * (1.0 - g0)), jnp.sum(weighted * diff, axis=0, keepdims=True)
 
 
-def shift_rows(dst, dst_row, dst_lane, src, src_row, count, start, width, chunk=64):
+def shift_all(dst, dst_lane, src, src_row, count, starts, width, chunk=64):
     def body(i, carry):
-        a = pl.multiple_of(src_row + i * chunk, chunk)
-        b = pl.multiple_of(dst_row + i * chunk, 16)
-        part = src[pl.ds(a, chunk), :]
-        dst[pl.ds(b, chunk), dst_lane : dst_lane + width] = part[:, start : start + width].astype(BF16)
+        part = src[pl.ds(pl.multiple_of(src_row + i * chunk, chunk), chunk), :]
+        for n, start in enumerate(starts):
+            row = pl.multiple_of(n * count + i * chunk, chunk)
+            dst[pl.ds(row, chunk), dst_lane : dst_lane + width] = part[:, start : start + width]
         return carry
 
     lax.fori_loop(0, count // chunk, body, 0)
 
 
-def weights_kernel(R, C, high, across, place, want, k1, k2, k3, w1, w1b, w2, w2b, k3t, masks, t1):
+def window(W, rows):
+    return [GUARD + i * W + j - 1 for i in range(rows) for j in range(3)]
+
+
+def weights_kernel(R, C, high, across, place, want, k1, k2, w1, w1b, w2_out, w2b_out, masks, t1, w2, w2b, sems):
     taps = k1.shape[0]
     ch1 = k1.shape[1]
     pick = lax.broadcasted_iota(jnp.int32, (768, taps), 0) == want[...]
@@ -111,23 +115,35 @@
             w2[pi * 2 * ch2 : (pi + 1) * 2 * ch2, a : a + 2 * ch1] = jnp.zeros((2 * ch2, 2 * ch1), BF16)
             a = (lane + 4 * x) * ch2
             w2b[pi * 2 * ch1 : (pi + 1) * 2 * ch1, a : a + 2 * ch2] = jnp.zeros((2 * ch1, 2 * ch2), BF16)
-    for y in range(size):
-        for pj in range(2):
+    copies = []
+    for pj in range(2):
+        for y in range(size):
             for x in range(3):
                 pair = jnp.concatenate([tap(y, 2 * x - pj), tap(y, 2 * x + 1 - pj)], axis=0).T.astype(BF16)
+                for pi in range(2):
+                    w = y + pi
+                    lane = ((w // 2) * 3 + x) * 4 + (w % 2) * 2
+                    row = (pi * 2 + pj) * ch2
+                    w2[row : row + ch2, lane * ch1 : (lane + 2) * ch1] = pair
+        for pi in range(2):
+            rows = pl.ds((pi * 2 + pj) * ch2, ch2)
+            copies.append(pltpu.make_async_copy(w2.at[rows], w2_out.at[rows], sems.at[len(copies)]))
+            copies[-1].start()
+    for pj in range(2):
+        for y in range(size):
+            for x in range(3):
                 back = jnp.concatenate(
                     [tap(size - 1 - y, size - 1 - 2 * x + pj), tap(size - 1 - y, size - 2 - 2 * x + pj)], axis=1
                 ).astype(BF16)
                 for pi in range(2):
                     w = y + pi
                     lane = ((w // 2) * 3 + x) * 4 + (w % 2) * 2
-                    row = (pi * 2 + pj) * ch2
-                    w2[row : row + ch2, lane * ch1 : (lane + 2) * ch1] = pair
                     row = (pi * 2 + pj) * ch1
                     w2b[row : row + ch1, lane * ch2 : (lane + 2) * ch2] = back
-    for k in range(0, 9, 2):
-        n = min(2, 9 - k) * ch2
-        k3t[:, k * ch2 : k * ch2 + n] = k3[k * ch2 : k * ch2 + n, :].astype(F32).T.astype(BF16)
+        for pi in range(2):
+            rows = pl.ds((pi * 2 + pj) * ch1, ch1)
+            copies.append(pltpu.make_async_copy(w2b.at[rows], w2b_out.at[rows], sems.at[len(copies)]))
+            copies[-1].start()
     W = C + 2 * HJ
     lane = lax.broadcasted_iota(jnp.int32, (1, masks.shape[1]), 1)
     i = ((lane.astype(F32) + 0.5) * (1.0 / W)).astype(jnp.int32)
@@ -145,6 +161,8 @@
             rows, columns = R * high, C * across
         ok = (i < count) & (r >= 0) & (r < rows) & (c >= 0) & (c < columns)
         masks[n : n + 1, :] = jnp.where(ok, 1.0, 0.0)
+    for copy in copies:
+        copy.wait()
 
 
 def cells_kernel(R, C, par, img, w1, b1, masks, pre, pool, msg_a, msg_b, sel, z, p1):
@@ -206,13 +224,13 @@
                 pool[row : row + quarter, :] = lanes_of(mine, 0, R * W, pool.shape[1]).astype(BF16)
 
 
-def first_grad_kernel(R, C, pre, lin, masks, w3, base, gain, loss, w3b):
+def first_grad_kernel(R, C, order, place, pre, lin, masks, b3, lin3, *refs):
+    k3, (base, gain, loss, w3, w3b, consts, bias) = refs[: len(order)], refs[len(order) :]
     frame = base.shape[3]
     ch = lin.shape[1]
+    c2 = w3b.shape[0]
     c3 = w3.shape[0]
-    c2 = w3b.shape[0]
-    for k in range(9):
-        w3b[:, k * c3 : (k + 1) * c3] = w3[:, (8 - k) * c2 : (9 - k) * c2].astype(F32).T.astype(BF16)
+    shard = k3[0].shape[1]
     total = jnp.zeros((1, frame), F32)
     weights = wide(column(lin), frame)
     for pi in range(2):
@@ -225,10 +243,23 @@
                 gain[pi, pj, t * ch : (t + 1) * ch, :] = 0.25 * slope
                 total = total + jnp.where(masks[1 + pi : 2 + pi, 0:frame] > 0.0, part, 0.0)
     loss[...] = jnp.broadcast_to(total, loss.shape)
+    bias[0] = column(b3)
+    bias[1] = column(lin3)
+    for n, flip in enumerate(order):
+        start = pl.multiple_of(jnp.bitwise_xor(place[2], flip) * shard, 8)
+        for e in range(2):
+            consts[e, n * shard : (n + 1) * shard, :] = bias[e, pl.ds(start, shard), :]
+        for k in range(0, 9, 2):
+            size = min(2, 9 - k) * c2
+            taps = k3[n][k * c2 : k * c2 + size, :].astype(F32)
+            w3[n * shard : (n + 1) * shard, k * c2 : k * c2 + size] = taps.T.astype(BF16)
+    for k in range(9):
+        taps = [k3[n][(8 - k) * c2 : (9 - k) * c2, :] for n in range(len(order))]
+        w3b[:, k * c3 : (k + 1) * c3] = jnp.concatenate(taps, axis=1)
 
 
 def middle_kernel(
-    R, C, par, pool, rec_a, rec_b, masks, w2, b2, lin2, w3, b3, lin3, w3b, d2, msg_a, msg_b, loss2, loss3,
+    R, C, pixels, par, pool, rec_a, rec_b, masks, w2, b2, lin2, w3, consts, w3b, loss1, d2, msg_a, msg_b, loss,
     s1, p2, pre2, q2, s2, p3, pre3, s3, p3b,
 ):
     W = C + 2 * HJ
@@ -238,7 +269,7 @@
     n4 = up128(R * W)
     c1 = pool.shape[0] // 2
     c2 = b2.shape[1]
-    c3 = b3.shape[1]
+    c3 = w3.shape[0]
     ext = s1.shape[1]
     inside = masks[3:4, 0 : (R + 6) * W]
     for r in range(0, 2 * c1, 64):
@@ -251,15 +282,13 @@
         whole = jnp.where(inside > 0.0, whole, 0.0)
         s1[r : r + 64, :] = jnp.concatenate(
             [jnp.zeros((64, GUARD), F32), whole, jnp.zeros((64, ext - GUARD - (R + 6) * W), F32)], axis=1
-        )
-    for k in range(9):
-        off = GUARD + (k // 3) * W + k % 3 - 1
-        for f in range(2):
-            shift_rows(p2, k * c1, f * n2, s1, f * c1, c1, off, n2)
+        ).astype(BF16)
+    for f in range(2):
+        shift_all(p2, f * n2, s1, f * c1, c1, window(W, 3), n2)
     tile = 256
     bias2 = column(b2, 4)
-    bias3 = column(b3)
-    lins3 = column(lin3)
+    bias3 = consts[0]
+    lins3 = consts[1]
 
     def second(t, carry):
         lanes = pl.ds(pl.multiple_of(t * tile, tile), tile)
@@ -274,13 +303,10 @@
     lax.fori_loop(0, 2 * n2 // tile, second, 0)
     for f in range(2):
         good = jnp.where(masks[4:5, 0:n2] > 0.0, q2[:, f * n2 : (f + 1) * n2], 0.0)
-        s2[f * c2 : (f + 1) * c2, 0:GUARD] = jnp.zeros((c2, GUARD), F32)
-        s2[f * c2 : (f + 1) * c2, GUARD : GUARD + n2] = good
-        s2[f * c2 : (f + 1) * c2, GUARD + n2 :] = jnp.zeros((c2, s2.shape[1] - GUARD - n2), F32)
-    for k in range(9):
-        off = GUARD + (k // 3) * W + k % 3 - 1
-        for f in range(2):
-            shift_rows(p3, k * c2, f * n3, s2, f * c2, c2, off, n3)
+        s2[f * c2 : (f + 1) * c2, 0:GUARD] = jnp.zeros((c2, GUARD), BF16)
+        s2[f * c2 : (f + 1) * c2, GUARD : GUARD + n2] = good.astype(BF16)
+        s2[f * c2 : (f + 1) * c2, GUARD + n2 :] = jnp.zeros((c2, s2.shape[1] - GUARD - n2), BF16)
+        shift_all(p3, f * n3, s2, f * c2, c2, window(W, 3), n3)
 
     def third(t, carry):
         lanes = pl.ds(pl.multiple_of(t * tile, tile), tile)
@@ -288,23 +314,22 @@
         return carry
 
     lax.fori_loop(0, 2 * n3 // tile, third, 0)
-    s3[:, 0:GUARD] = jnp.zeros((c3, GUARD), F32)
-    s3[:, GUARD + n3 :] = jnp.zeros((c3, s3.shape[1] - GUARD - n3), F32)
+    s3[:, 0:GUARD] = jnp.zeros((c3, GUARD), BF16)
+    s3[:, GUARD + n3 :] = jnp.zeros((c3, s3.shape[1] - GUARD - n3), BF16)
     total = jnp.zeros((1, 128), F32)
     for t in range(n3 // 128):
         v0 = pre3[:, t * 128 : (t + 1) * 128]
         v1 = pre3[:, n3 + t * 128 : n3 + (t + 1) * 128]
         dfeat, slope, part = layer_terms(v0, v1, lins3, 256.0)
         lanes = slice(t * 128, (t + 1) * 128)
-        s3[:, GUARD + t * 128 : GUARD + (t + 1) * 128] = jnp.where(masks[5:6, lanes] > 0.0, dfeat * slope, 0.0)
+        d = jnp.where(masks[5:6, lanes] > 0.0, dfeat * slope, 0.0)
+        s3[:, GUARD + t * 128 : GUARD + (t + 1) * 128] = d.astype(BF16)
         total = total + jnp.where(masks[6:7, lanes] > 0.0, part, 0.0)
-    loss3[...] = jnp.broadcast_to(total, loss3.shape)
-    for k in range(9):
-        off = GUARD + (k // 3) * W + k % 3 - 1
-        shift_rows(p3b, k * c3, 0, s3, 0, c3, off, n4)
+    shift_all(p3b, 0, s3, 0, c3, window(W, 3), n4)
     up = 0.25 * jnp.dot(w3b[...], p3b[...], preferred_element_type=F32)
     total2 = jnp.zeros((1, n4), F32)
     weights = wide(column(lin2), n4)
+    strips = []
     for t in range(4):
         rows = slice(t * c2, (t + 1) * c2)
         v0 = pre2[rows, 0:n2][:, 2 * W : 2 * W + n4]
@@ -313,16 +338,32 @@
         d = jnp.where(masks[0:1, 0:n4] > 0.0, (dfeat + up) * slope, 0.0)
         d2[rows, :] = d.astype(BF16)
         total2 = total2 + jnp.where(masks[7:8, 0:n4] > 0.0, part, 0.0)
-        head = lanes_of(d, 0, 2 * W, msg_a.shape[1])
-        tail = lanes_of(d, (R - 2) * W, 2 * W, msg_a.shape[1])
+        strips.append(d)
+    rest = jnp.zeros((c2, msg_a.shape[1] - 3 * W), F32)
+    for pj in range(2):
+        upper, lower = strips[pj], strips[2 + pj]
+        head = jnp.concatenate([upper[:, 0:W], lower[:, 0:W], upper[:, W : 2 * W], rest], axis=1)
+        tail = jnp.concatenate(
+            [lower[:, (R - 2) * W : (R - 1) * W], upper[:, (R - 1) * W : R * W], lower[:, (R - 1) * W : R * W], rest],
+            axis=1,
+        )
+        rows = slice(pj * c2, (pj + 1) * c2)
         msg_a[rows, :] = jnp.where(even, tail, head).astype(BF16)
         msg_b[rows, :] = jnp.where(even, head, tail).astype(BF16)
-    loss2[...] = jnp.broadcast_to(total2, loss2.shape)
+    each = (
+        jnp.sum(loss1[0:1, :]) / (pixels // 16) + jnp.sum(total2) / (pixels // 64) + jnp.sum(total) / (pixels // 256)
+    )
+    loss[...] = jnp.full(loss.shape, each, F32)
 
 
 def last_kernel(
-    R, C, par, d2, rec_a, rec_b, masks, w2b, base, gain, w1b, out, s4, p2b, s5, p1b, g, sel, flat
+    R, C, par, d2, rec_a, rec_b, masks, w2b_in, base_in, gain_in, w1b_in, out,
+    s4, p2b, s5, p1b, g, sel, flat, w2b, base, gain, w1b, sems,
 ):
+    pairs = ((w2b_in, w2b), (base_in, base), (gain_in, gain), (w1b_in, w1b))
+    fetch = [pltpu.make_async_copy(a, b, sems.at[n]) for n, (a, b) in enumerate(pairs)]
+    for copy in fetch:
+        copy.start()
     W = C + 2 * HJ
     even = lax.rem(par[0], 2) == 0
     c2 = d2.shape[0]
@@ -332,26 +373,29 @@
     ch = w2b.shape[0] // 4
     inside = masks[4:5, 0 : (R + 4) * W]
 
-    def join(i, carry):
-        rows = pl.ds(pl.multiple_of(i * 64, 64), 64)
-        a = rec_a[rows, :].astype(F32)
-        b = rec_b[rows, :].astype(F32)
-        above = jnp.where(even, b, a)[:, 0 : 2 * W]
-        below = jnp.where(even, a, b)[:, 0 : 2 * W]
-        mine = d2[rows, :].astype(F32)[:, 0 : R * W]
-        whole = jnp.concatenate([above, mine, below], axis=1)
-        whole = jnp.where(inside > 0.0, whole, 0.0)
-        s4[rows, :] = jnp.concatenate(
+    none = jnp.zeros((64, W), F32)
+    for t in range(0, c2, 64):
+        pi, row = t // (c2 // 2), t % (c2 // 2)
+        a = rec_a[row : row + 64, :].astype(F32)
+        b = rec_b[row : row + 64, :].astype(F32)
+        above = jnp.where(even, b, a)
+        below = jnp.where(even, a, b)
+        strips = [[v[:, n * W : (n + 1) * W] for n in range(3)] for v in (above, below)]
+        mine = d2[t : t + 64, :].astype(F32)[:, 0 : R * W]
+        if pi == 0:
+            parts = [none, strips[0][1], mine, strips[1][0], strips[1][2]]
+        else:
+            parts = [strips[0][0], strips[0][2], mine, strips[1][1], none]
+        whole = jnp.where(inside > 0.0, jnp.concatenate(parts, axis=1), 0.0)
+        s4[t : t + 64, :] = jnp.concatenate(
             [jnp.zeros((64, GUARD), F32), whole, jnp.zeros((64, ext - GUARD - (R + 4) * W), F32)], axis=1
-        )
-        return carry
-
-    lax.fori_loop(0, c2 // 64, join, 0)
+        ).astype(BF16)
+    shift_all(p2b, 0, s4, 0, c2, window(W, 4), frame)
+    for copy in fetch:
+        copy.wait()
     for qi in range(2):
-        for k in range(9):
-            off = GUARD + (k // 3 + 1 - qi) * W + k % 3 - 1
-            shift_rows(p2b, k * c2, 0, s4, 0, c2, off, frame)
-        up = jnp.dot(w2b[qi * 2 * ch : (qi + 1) * 2 * ch, :], p2b[...], preferred_element_type=F32)
+        around = p2b[(1 - qi) * 3 * c2 : (4 - qi) * 3 * c2, :]
+        up = jnp.dot(w2b[qi * 2 * ch : (qi + 1) * 2 * ch, :], around, preferred_element_type=F32)
         good = masks[8 + qi : 9 + qi, 0:frame] > 0.0
         for qj in range(2):
             part = up[qj * ch : (qj + 1) * ch]
@@ -359,9 +403,9 @@
                 rows = slice(t * ch, (t + 1) * ch)
                 d = base[qi, qj, rows, :] + gain[qi, qj, rows, :] * part
                 row = ((qi * 2 + qj) * 4 + t) * ch
-                s5[row : row + ch, 0:GUARD] = jnp.zeros((ch, GUARD), F32)
-                s5[row : row + ch, GUARD : GUARD + frame] = jnp.where(good, d, 0.0)
-                s5[row : row + ch, GUARD + frame :] = jnp.zeros((ch, s5.shape[1] - GUARD - frame), F32)
+                s5[row : row + ch, 0:GUARD] = jnp.zeros((ch, GUARD), BF16)
+                s5[row : row + ch, GUARD : GUARD + frame] = jnp.where(good, d, 0.0).astype(BF16)
+                s5[row : row + ch, GUARD + frame :] = jnp.zeros((ch, s5.shape[1] - GUARD - frame), BF16)
     for qi in range(2):
         for qj in range(2):
             for wi in range(4):
@@ -373,7 +417,7 @@
                     off = GUARD + (dy + y // 2) * W + dx
                     p1b[(wi * 4 + wj) * ch : (wi * 4 + wj + 1) * ch, :] = s5[row : row + ch, :][
                         :, off : off + n4
-                    ].astype(BF16)
+                    ]
             g[qi, qj] = jnp.dot(w1b[...], p1b[...], preferred_element_type=F32)
     for s in range(0, S, 2):
         for c in range(3):
@@ -424,15 +468,29 @@
     return before, after
 
 
-def call(kernel, outs, scratch, *args):
-    specs = [pl.BlockSpec(memory_space=pltpu.SMEM if a.ndim == 1 else pltpu.VMEM) for a in args]
+class Far:
+    def __init__(self, array):
+        self.array = array
+
+
+def call(kernel, outs, scratch, limit, work, *args, far=()):
+    def place(a):
+        if isinstance(a, Far):
+            return pltpu.HBM
+        return pltpu.SMEM if a.ndim == 1 else pltpu.VMEM
+
+    specs = [pl.BlockSpec(memory_space=place(a)) for a in args]
+    args = [a.array if isinstance(a, Far) else a for a in args]
+    spaces = [pltpu.HBM if n in far else pltpu.VMEM for n in range(len(jax.tree.leaves(outs)))]
+    out_specs = jax.tree.unflatten(jax.tree.structure(outs), [pl.BlockSpec(memory_space=m) for m in spaces])
     return pl.pallas_call(
         kernel,
         out_shape=outs,
         in_specs=specs,
-        out_specs=jax.tree.map(lambda _: pl.BlockSpec(memory_space=pltpu.VMEM), outs),
+        out_specs=out_specs,
         scratch_shapes=scratch,
-        compiler_params=pltpu.CompilerParams(vmem_limit_bytes=56 * 2**20),
+        compiler_params=pltpu.CompilerParams(vmem_limit_bytes=limit * 2**20),
+        cost_estimate=pl.CostEstimate(flops=work * 10**9, bytes_accessed=2**20, transcendentals=0),
     )(*args)
 
 
@@ -450,6 +508,41 @@
     pixels = image_gen.shape[1] * image_gen.shape[2] * high * across
     ch1, ch2, ch3 = bias_one.shape[0], bias_two.shape[0], bias_three.shape[0]
 
+    y, x, c, a, b = np.meshgrid(*(np.arange(n) for n in (3, 3, 3, 4, 4)), indexing="ij")
+    want = jnp.asarray((x * 192 + b * 48 + c * 16 + y * 4 + a).reshape(1, -1), jnp.int32)
+    place = jnp.stack([at_row, at_col, lax.axis_index("chan")]).astype(jnp.int32)
+    shard = kernel_three.shape[3]
+
+    def arr(shape, dtype=F32):
+        return jax.ShapeDtypeStruct(shape, dtype)
+
+    w1, w1b, w2, w2b, masks = call(
+        functools.partial(weights_kernel, R, C, high, across),
+        (
+            arr((4 * ch1, 768), BF16),
+            arr((192, 16 * ch1), BF16),
+            arr((4 * ch2, 36 * ch1), BF16),
+            arr((4 * ch1, 36 * ch2), BF16),
+            arr((16, 1024)),
+        ),
+        [
+            pltpu.VMEM((976, ch1), F32),
+            pltpu.VMEM((4 * ch2, 36 * ch1), BF16),
+            pltpu.VMEM((4 * ch1, 36 * ch2), BF16),
+            pltpu.SemaphoreType.DMA((8,)),
+        ],
+        62, 5, place, want, kernel_one.reshape(-1, ch1), kernel_two, far=(2, 3),
+    )
+    parts = lax.axis_size("chan")
+    pieces = [kernel_three.reshape(-1, shard)]
+    order = [0]
+    step = parts // 2
+    while step > 0:
+        pairs = [(i, i ^ step) for i in range(parts)]
+        pieces = pieces + [lax.ppermute(piece, "chan", pairs) for piece in pieces]
+        order = order + [n ^ step for n in order]
+        step //= 2
+
     offsets = jnp.array(OFFSETS, F32)[:, None, None]
     spreads = jnp.array(SPREADS, F32)[:, None, None]
     both = jnp.stack([((image - offsets) / spreads).astype(BF16) for image in (image_gen, image_ref)])
@@ -461,38 +554,6 @@
     rim = jnp.pad(rim, ((0, 0), (0, 0), (0, 0), (0, span - W * S)))
     rim = rim.reshape(2, 3 * (R * S + 2 * RIM), span)
 
-    y, x, c, a, b = np.meshgrid(*(np.arange(n) for n in (3, 3, 3, 4, 4)), indexing="ij")
-    want = jnp.asarray((x * 192 + b * 48 + c * 16 + y * 4 + a).reshape(1, -1), jnp.int32)
-    place = jnp.stack([at_row, at_col]).astype(jnp.int32)
-    shard = kernel_three.shape[3]
-
-    def arr(shape, dtype=F32):
-        return jax.ShapeDtypeStruct(shape, dtype)
-
-    w1, w1b, w2, w2b, mine, masks = call(
-        functools.partial(weights_kernel, R, C, high, across),
-        (
-            arr((4 * ch1, 768), BF16),
-            arr((192, 16 * ch1), BF16),
-            arr((4 * ch2, 36 * ch1), BF16),
-            arr((4 * ch1, 36 * ch2), BF16),
-            arr((shard, 9 * ch2), BF16),
-            arr((16, 1024)),
-        ),
-        [pltpu.VMEM((976, ch1), F32)],
-        place, want, kernel_one.reshape(-1, ch1), kernel_two, kernel_three.reshape(-1, shard),
-    )
-    parts = lax.axis_size("chan")
-    whole = mine[None]
-    step = 1
-    here = lax.axis_index("chan")
-    while step < parts:
-        other = lax.ppermute(whole, "chan", [(i, i ^ step) for i in range(parts)])
-        first = (here & step) == 0
-        whole = jnp.concatenate([jnp.where(first, whole, other), jnp.where(first, other, whole)])
-        step *= 2
-    w3 = whole.reshape(ch3, 9 * ch2)
-
     def flat(values):
         return values.reshape(1, -1)
 
@@ -512,60 +573,63 @@
             arr((8 * ch1, up128(3 * W)), BF16),
         ),
         [pltpu.VMEM((span, span), BF16), pltpu.VMEM((2, rows, span), F32), pltpu.VMEM((768, 2 * frame), BF16)],
-        place, rim, w1, b1, masks,
+        18, 5, place, rim, w1, b1, masks,
     )
     rec_a, rec_b = swap(msg_a, msg_b, ROWS)
-    base, gain, loss1, w3b = call(
-        functools.partial(first_grad_kernel, R, C),
-        (arr((2, 2, 4 * ch1, frame)), arr((2, 2, 4 * ch1, frame)), arr((8, frame)), arr((ch2, 9 * ch3), BF16)),
-        [],
-        pre, lin1, masks, w3,
+    base, gain, loss1, w3, w3b, consts = call(
+        functools.partial(first_grad_kernel, R, C, tuple(order)),
+        (arr((2, 2, 4 * ch1, frame)), arr((2, 2, 4 * ch1, frame)), arr((8, frame)),
+            arr((ch3, 9 * ch2), BF16), arr((ch2, 9 * ch3), BF16), arr((2, ch3, 128))),
+        [pltpu.VMEM((2, ch3, 128), F32)],
+        12, 3, place, pre, lin1, masks, b3, lin3, *pieces,
     )
     ext1 = GUARD + up128((R + 6) * W) + GUARD
-    d2, msg_a, msg_b, loss2, loss3 = call(
-        functools.partial(middle_kernel, R, C),
+    everyone = high * across
+    d2, msg_a, msg_b, each = call(
+        functools.partial(middle_kernel, R, C, pixels),
         (
             arr((4 * ch2, n4), BF16),
-            arr((4 * ch2, up128(2 * W)), BF16),
-            arr((4 * ch2, up128(2 * W)), BF16),
-            arr((8, n4)),
-            arr((8, 128)),
+            arr((2 * ch2, up128(3 * W)), BF16),
+            arr((2 * ch2, up128(3 * W)), BF16),
+            arr((everyone, 8, 128)),
         ),
         [
-            pltpu.VMEM((8 * ch1, ext1), F32),
+            pltpu.VMEM((8 * ch1, ext1), BF16),
             pltpu.VMEM((36 * ch1, 2 * n2), BF16),
             pltpu.VMEM((4 * ch2, 2 * n2), F32),
             pltpu.VMEM((ch2, 2 * n2), F32),
-            pltpu.VMEM((2 * ch2, GUARD + n2 + GUARD), F32),
+            pltpu.VMEM((2 * ch2, GUARD + n2 + GUARD), BF16),
             pltpu.VMEM((9 * ch2, 2 * n3), BF16),
             pltpu.VMEM((ch3, 2 * n3), F32),
-            pltpu.VMEM((ch3, GUARD + n3 + GUARD), F32),
+            pltpu.VMEM((ch3, GUARD + n3 + GUARD), BF16),
             pltpu.VMEM((9 * ch3, n4), BF16),
         ],
-        place, pool, rec_a, rec_b, masks, w2, b2, lin2, w3, b3, lin3, w3b,
+        30, 10, place, pool, rec_a, rec_b, masks, w2, b2, lin2, w3, consts, w3b, loss1,
     )
     rec_a, rec_b = swap(msg_a, msg_b, ROWS)
-    partial_loss = (
-        jnp.sum(loss1[0]) / (pixels // 16) + jnp.sum(loss2[0]) / (pixels // 64) + jnp.sum(loss3[0]) / (pixels // 256)
-    )
-    everyone = high * across
-    spread_out = jnp.broadcast_to(partial_loss, (everyone, 8, 128))
-    loss = jnp.sum(lax.all_to_all(spread_out, ("row", "col", "chan"), 0, 0)[:, 0, 0])
+    with jax.named_scope("share"):
+        everywhere = lax.all_to_all(each, ("row", "col", "chan"), 0, 0)
     image_grad = call(
         functools.partial(last_kernel, R, C),
         arr(image_gen.shape),
         [
-            pltpu.VMEM((4 * ch2, GUARD + up128((R + 4) * W) + GUARD), F32),
-            pltpu.VMEM((36 * ch2, frame), BF16),
-            pltpu.VMEM((16 * ch1, GUARD + frame + GUARD), F32),
+            pltpu.VMEM((4 * ch2, GUARD + up128((R + 4) * W) + GUARD), BF16),
+            pltpu.VMEM((48 * ch2, frame), BF16),
+            pltpu.VMEM((16 * ch1, GUARD + frame + GUARD), BF16),
             pltpu.VMEM((16 * ch1, n4), BF16),
             pltpu.VMEM((2, 2, 192, n4), F32),
             pltpu.VMEM((S * C, S * C), BF16),
             pltpu.VMEM((3 * R * S, S * C), F32),
+            pltpu.VMEM(w2b.shape, BF16),
+            pltpu.VMEM(base.shape, F32),
+            pltpu.VMEM(gain.shape, F32),
+            pltpu.VMEM(w1b.shape, BF16),
+            pltpu.SemaphoreType.DMA((4,)),
         ],
-        place, d2, rec_a, rec_b, masks, w2b, base, gain, w1b,
-    )
-    return image_grad, loss
+        62, 10, place, d2, rec_a, rec_b, masks, Far(w2b), Far(base), Far(gain), Far(w1b),
+    )
+    everywhere, image_grad = lax.optimization_barrier((everywhere, image_grad))
+    return image_grad, jnp.sum(everywhere[:, 0, 0])
 
 
 def solution(mesh):

time: 134 us -> 82.4 us (0.61)
  Pallas kernels: 81.6 us -> 46.1 us
  blocking collectives: 11.1 us -> 0 us
  other arithmetic: 9.9 us -> 6.32 us
  waiting for transfers between devices: 8.12 us -> 5.42 us
  between operations: 2.84 us -> 0.9 us
  local copies, waits for them, and re-layouts: 4.15 us -> 5.8 us
    pallas_call x5, Pallas kernels: 81.6 us -> 46.1 us  [call(): pl.pallas_call(kernel, out_shape=outs, in_specs=specs, out_specs=out_spec...]
    all_to_all x1 -> x0, blocking collectives: 11.1 us -> none  [local(): lax.all_to_all(spread_out, ('row', 'col', 'chan'), 0, 0)[:, 0, 0]]
    reduce_sum x4 -> x1, other arithmetic: 4.71 us -> 0.63 us  [local(): return (image_grad, jnp.sum(everywhere[:, 0, 0]))]
    all_to_all x0 -> x1, starting transfers between devices: none -> 2.79 us  [local(): everywhere = lax.all_to_all(each, ('row', 'col', 'chan'), 0, 0)]
    ppermute x2 -> x3, starting transfers between devices: 1.65 us -> 4.43 us  [local(): pieces = pieces + [lax.ppermute(piece, 'chan', pairs) for piece in pieces]]
    ppermute x4, starting transfers between devices: 10.6 us -> 8.21 us  [swap(): return (first, lax.ppermute(b, axis, second))]
    ppermute x4, starting transfers between devices: 3.52 us -> 1.22 us  [swap(): first = lax.ppermute(a, axis, [(i, i ^ 1) for i in range(count)])]
    unnamed x20 -> x32, local copies, waits for them, and re-layouts: 1.82 us -> 3.92 us
  transfers between devices with their start and end apart: 10 -> 12, of which waited for: 4 -> 4; matrix products, arithmetic and copies ran while one was open for 7% -> 9% of each run, Pallas kernels for 12% -> 33%
where the time goes in v1:
time: 82.4 us; the launch traced here: 81.2 us
  Pallas kernels  46.1 us (56%)
  starting transfers between devices  16.6 us (20%)
  other arithmetic  6.32 us (8%)
  local copies, waits for them, and re-layouts  5.8 us (7%)
  waiting for transfers between devices  5.42 us (7%)
  between operations  0.9 us (1%)
    pallas_call x5, Pallas kernels, call(): pl.pallas_call(kernel, out_shape=outs, in_specs=specs, out_specs=out_spec...  46.1 us
    ppermute x4, starting transfers between devices, swap(): return (first, lax.ppermute(b, axis, second))  8.21 us
    ppermute x3, starting transfers between devices, local(): pieces = pieces + [lax.ppermute(piece, 'chan', pairs) for piece in pieces]  4.43 us
    ppermute x4, waiting for transfers between devices, swap(): return (first, lax.ppermute(b, axis, second))  3.99 us
    unnamed x32, local copies, waits for them, and re-layouts  3.92 us
    all_to_all x1, starting transfers between devices, local(): everywhere = lax.all_to_all(each, ('row', 'col', 'chan'), 0, 0)  2.79 us
    another operation x2, other arithmetic, local(): jnp.stack([((image - offsets) / spreads).astype(BF16) for image in (image...  2.6 us
    concatenate x1, local copies, waits for them, and re-layouts, local(): rim = jnp.concatenate([left, both, right], axis=3)  1.88 us
  transfers between devices with their start and end apart: 12, of which 4 were waited for; matrix products, arithmetic and copies ran while one was open for 9% of the time, Pallas kernels for 33%

profile of v1, /device:TPU:0, one launch (start us, length us, event | category | flops | bytes accessed | tf_op | source)
XLA Modules:
  0.0 81.2 jit_solution(7589730668535444750)
XLA Ops:
  0.6 0.6 collective-permute-start.7
  1.2 2.6 %collective-permute-start.6 = (bf16[1728,96]{1,0:T(8,128)(2,1)}, bf16[1728,96]{1,0:T(8,128)(2,1)S(1)}, u32[]{:S(2)}, u32[]{:S(2)}) collective-permute-start(bf16[1728,96]{1,0:T(8,128)(2,1)} %bitcast.16), channel_id=1, source_target_pairs={{0,2},{1,3},{2,0},{3,1},{4,6},{5,7},{6,4},{7,5},{8,10},{9,11},{10,... | collective-permute-start | bytes 995336 | tf_op jit(solution)/shard_map/ppermute | solution.py:542
  3.8 1.7 %fusion.5 = (bf16[1,3,64,1024]{3,2,1,0:T(8,128)(2,1)S(1)}, bf16[1,3,64,1024]{3,2,1,0:T(8,128)(2,1)S(1)}) fusion(f32[3,64,1024]{2,1,0:T(8,128)} %param.14, f32[3]{0:T(128)} %constant.54, f32[3]{0:T(128)} %constant.56, f32[3,64,1024]{2,1,0:T(8,128)} %param.15), kind=kLoop, calls=%fused_computation.13 | loop fusion | flops 1179648 | bytes 2359320 | tf_op jit(solution)/shard_map/stack | solution.py:548
  5.4 0.1 broadcast_select_fusion.2
  5.6 3.7 %collective-permute-start = (bf16[2,3,64,96]{3,2,1,0:T(8,128)(2,1)S(1)}, bf16[2,3,64,96]{3,2,1,0:T(8,128)(2,1)S(1)}, u32[]{:S(2)}, u32[]{:S(2)}) collective-permute-start(bf16[2,3,64,96]{3,2,1,0:T(8,128)(2,1)S(1)} %broadcast_select_fusion.3), channel_id=1, source_target_pairs={{4,8},{12,0},{8,4},{0,12},{5,9},{13,1},{9,5},{1,13},{6,10},{14,2},... | collective-permute-start | bytes 221192 | tf_op jit(solution)/shard_map/ppermute | solution.py:456
  9.2 0.9 %pad_maximum_fusion = bf16[2,3,64,1024]{3,2,1,0:T(8,128)(2,1)} fusion(bf16[1,3,64,1024]{3,2,1,0:T(8,128)(2,1)S(1)} %get-tuple-element.54, bf16[1,3,64,1024]{3,2,1,0:T(8,128)(2,1)S(1)} %get-tuple-element.53), kind=kLoop, calls=%fused_computation.8 | loop fusion | flops 393216 | bytes 1572864 | tf_op jit(solution)/shard_map/stack | solution.py:548
  10.2 0.6 pad_add_fusion.place.par
  10.8 2.3 %collective-permute-done = bf16[2,3,64,96]{3,2,1,0:T(8,128)(2,1)S(1)} collective-permute-done((bf16[2,3,64,96]{3,2,1,0:T(8,128)(2,1)S(1)}, bf16[2,3,64,96]{3,2,1,0:T(8,128)(2,1)S(1)}, u32[]{:S(2)}, u32[]{:S(2)}) %collective-permute-start) | collective-permute-done | bytes 73760 | tf_op jit(solution)/shard_map/ppermute | solution.py:456
  13.1 1.4 %collective-permute-done.1 = bf16[2,3,64,96]{3,2,1,0:T(8,128)(2,1)S(1)} collective-permute-done((bf16[2,3,64,96]{3,2,1,0:T(8,128)(2,1)S(1)}, bf16[2,3,64,96]{3,2,1,0:T(8,128)(2,1)S(1)}, u32[]{:S(2)}, u32[]{:S(2)}) %collective-permute-start.1) | collective-permute-done | bytes 73760 | tf_op jit(solution)/shard_map/ppermute | solution.py:453
  14.6 1.9 %concatenate.6 = bf16[2,3,64,1216]{3,2,1,0:T(8,128)(2,1)S(1)} concatenate(bf16[2,3,64,96]{3,2,1,0:T(8,128)(2,1)S(1)} %get-tuple-element.52, bf16[2,3,64,1024]{3,2,1,0:T(8,128)(2,1)} %pad_maximum_fusion, bf16[2,3,64,96]{3,2,1,0:T(8,128)(2,1)S(1)} %get-tuple-element.51), dimensions={3} | concatenate | bytes 1867776 | tf_op jit(solution)/shard_map/concatenate | solution.py:550
  16.5 0.9 %broadcast_select_fusion.1 = (bf16[2,3,12,1216]{3,2,1,0:T(8,128)(2,1)}, bf16[2,3,12,1216]{3,2,1,0:T(8,128)(2,1)}) fusion(pred[]{:T(512)S(6)} %eq.9, bf16[2,3,64,1216]{3,2,1,0:T(8,128)(2,1)S(1)} %concatenate.6), kind=kLoop, calls=%fused_computation.18 | loop fusion | flops 175104 | bytes 700417 | tf_op jit(solution)/shard_map/jit(_where)/select_n | solution.py:464
  17.3 0.6 collective-permute-start.2
  17.9 5.9 %shard_map.149 = (bf16[256,768]{1,0:T(8,128)(2,1)}, bf16[192,1024]{1,0:T(8,128)(2,1)}, bf16[768,2304]{1,0:T(8,128)(2,1)}, bf16[256,6912]{1,0:T(8,128)(2,1)}, f32[16,1024]{1,0:T(8,128)}) custom-call(s32[3]{0:T(128)} %pad_add_fusion.place.par, s32[1,432]{1,0:T(1,128)} %constant.49.clone.want, bf16[432,64]{1,0:T(8,128)(2,1)} %bitcast.22, bf16[5,5,64,192]{3,2,1,0:T(8,128)(2,1)} %k2.1), custom_call_target="tpu_custom_call" | custom-call | flops 5000000000 | bytes 1048576 | tf_op jit(solution)/shard_map/pallas_call | solution.py:486
  23.9 0.3 collective-permute-done.2
  24.3 1.1 %select_select_fusion.1 = (bf16[2,3,12,1216]{3,2,1,0:T(8,128)(2,1)S(1)}, bf16[2,3,12,1216]{3,2,1,0:T(8,128)(2,1)S(1)}) fusion(bf16[2,3,12,1216]{3,2,1,0:T(8,128)(2,1)} %collective-permute-done.2, bf16[2,3,12,1216]{3,2,1,0:T(8,128)(2,1)} %collective-permute-done.3, pred[]{:T(512)S(6)} %eq.9, pred[]{:T(512)S(6)} %gt.6, pred[]{:T(512)S(6)} %lt.19), kind=kLoop, calls=%fused_computation.16 | loop fusion | flops 350208 | bytes 700419 | tf_op jit(solution)/shard_map/jit(_where)/select_n | solution.py:466
  25.4 0.4 fusion.4
  25.8 1.3 %collective-permute-start.8 = (bf16[1728,96]{1,0:T(8,128)(2,1)S(1)}, bf16[1728,96]{1,0:T(8,128)(2,1)S(1)}, u32[]{:S(2)}, u32[]{:S(2)}) collective-permute-start(bf16[1728,96]{1,0:T(8,128)(2,1)S(1)} %collective-permute-done.6.refs_1_), channel_id=1, source_target_pairs={{0,1},{1,0},{2,3},{3,2},{4,5},{5,4},{6,7},{7,6},{8,9},{9,8},{10,11... | collective-permute-start | bytes 995336 | tf_op jit(solution)/shard_map/ppermute | solution.py:542
  27.1 6.3 %shard_map.150 = (f32[2,2,256,768]{3,2,1,0:T(8,128)S(1)}, bf16[512,384]{1,0:T(8,128)(2,1)S(1)}, bf16[512,256]{1,0:T(8,128)(2,1)S(1)}, bf16[512,256]{1,0:T(8,128)(2,1)S(1)}) custom-call(s32[3]{0:T(128)S(1)} %copy-done, bf16[2,264,1280]{2,1,0:T(8,128)(2,1)S(1)} %bitcast.14, bf16[256,768]{1,0:T(8,128)(2,1)S(1)} %copy-done.10, f32[1,64]{1,0:T(1,128)S(1)} %bitcast.20, ...), custom_call_target="tpu_custom_call" | custom-call | flops 5000000000 | bytes 1048576 | tf_op jit(solution)/shard_map/pallas_call | solution.py:486
  33.5 0.6 collective-permute-start.4
  34.0 2.0 %collective-permute-start.5 = (bf16[512,256]{1,0:T(8,128)(2,1)S(1)}, bf16[512,256]{1,0:T(8,128)(2,1)S(1)}, u32[]{:S(2)}, u32[]{:S(2)}) collective-permute-start(bf16[512,256]{1,0:T(8,128)(2,1)S(1)} %get-tuple-element.27), channel_id=1, source_target_pairs={{1,2},{3,16},{17,18},{19,0},{2,1},{16,3},{18,17},{0,19},{5,6},{7,2... | collective-permute-start | bytes 786440 | tf_op jit(solution)/shard_map/ppermute | solution.py:456
  36.1 3.7 %shard_map.151 = (f32[2,2,256,384]{3,2,1,0:T(8,128)S(1)}, f32[2,2,256,384]{3,2,1,0:T(8,128)S(1)}, f32[8,384]{1,0:T(8,128)S(1)}, bf16[384,1728]{1,0:T(8,128)(2,1)...) custom-call(s32[3]{0:T(128)S(1)} %copy-done, f32[2,2,256,768]{3,2,1,0:T(8,128)S(1)} %get-tuple-element.29.pre, ...), custom_call_target="tpu_custom_call" | custom-call | flops 3000000000 | bytes 1048576 | tf_op jit(solution)/shard_map/pallas_call | solution.py:486
  39.7 1.2 %copy-done.6 = f32[2,2,256,384]{3,2,1,0:T(8,128)} copy-done((f32[2,2,256,384]{3,2,1,0:T(8,128)}, f32[2,2,256,384]{3,2,1,0:T(8,128)S(1)}, u32[]{:S(2)}) %copy-start.6) | copy-done | bytes 1572888
  40.9 1.1 %copy-done.7 = f32[2,2,256,384]{3,2,1,0:T(8,128)} copy-done((f32[2,2,256,384]{3,2,1,0:T(8,128)}, f32[2,2,256,384]{3,2,1,0:T(8,128)S(1)}, u32[]{:S(2)}) %copy-start.7) | copy-done | bytes 1572888
  42.1 19.1 %shard_map.152 = (bf16[768,384]{1,0:T(8,128)(2,1)S(1)}, bf16[384,256]{1,0:T(8,128)(2,1)S(1)}, bf16[384,256]{1,0:T(8,128)(2,1)S(1)}, f32[32,8,128]{2,1,0:T(8,128)}) custom-call(s32[3]{0:T(128)S(1)} %copy-done, bf16[512,384]{1,0:T(8,128)(2,1)S(1)} %get-tuple-element.25.pool, bf16[512,256]{1,0:T(8,128)(2,1)S(1)} %collective-permute-done.4.rec_a, ...), custom_call_target="tpu_custom_call" | custom-call | flops 10000000000 | bytes 1048576 | tf_op jit(solution)/shard_map/pallas_call | solution.py:486
  61.2 0.8 copy-done.11
  62.0 0.6 collective-permute-start.9
  62.6 2.0 %collective-permute-start.10 = (bf16[384,256]{1,0:T(8,128)(2,1)S(1)}, bf16[384,256]{1,0:T(8,128)(2,1)S(1)}, u32[]{:S(2)}, u32[]{:S(2)}) collective-permute-start(bf16[384,256]{1,0:T(8,128)(2,1)S(1)} %get-tuple-element.37), channel_id=1, source_target_pairs={{1,2},{3,16},{17,18},{19,0},{2,1},{16,3},{18,17},{0,19},{5,6},{7,2... | collective-permute-start | bytes 589832 | tf_op jit(solution)/shard_map/ppermute | solution.py:456
  64.6 2.8 %all-to-all-start = ((f32[32,8,128]{2,1,0:T(8,128)}), f32[32,8,128]{2,1,0:T(8,128)S(1)}, u32[]{:S(2)}, u32[]{:S(2)}) async-start(f32[32,8,128]{2,1,0:T(8,128)} %get-tuple-element.34), calls=%async_computation | async-start | bytes 262144 | tf_op jit(solution)/shard_map/share/all_to_all | solution.py:611
  67.4 1.3 %collective-permute-done.10.rec_b = bf16[384,256]{1,0:T(8,128)(2,1)S(1)} collective-permute-done((bf16[384,256]{1,0:T(8,128)(2,1)S(1)}, bf16[384,256]{1,0:T(8,128)(2,1)S(1)}, u32[]{:S(2)}, u32[]{:S(2)}) %collective-permute-start.10) | collective-permute-done | bytes 196640 | tf_op jit(solution)/shard_map/ppermute | solution.py:456
  68.7 0.7 copy-done.15
  69.4 11.2 %shard_map.153 = f32[3,64,1024]{2,1,0:T(8,128)} custom-call(s32[3]{0:T(128)} %pad_add_fusion.place.par, bf16[768,384]{1,0:T(8,128)(2,1)} %copy-done.11, bf16[384,256]{1,0:T(8,128)(2,1)} %copy-done.14, bf16[384,256]{1,0:T(8,128)(2,1)} %copy-done.15, f32[16,1024]{1,0:T(8,128)} %get-tuple-element.24.masks, bf16[256,6912]{1,0:T(8,128)(2,1)} %get-tuple-element.38.w2b_in, ...), custom_call_target="tpu_custom_call" | custom-call | flops 10000000000 | bytes 1048576 | tf_op jit(solution)/shard_map/pallas_call | solution.py:486
  80.6 0.6 slice_reduce_fusion
  (42 shorter events, 0.1 us)
Async XLA Ops:
  0.6 35.4 %collective-permute-start.7 = (bf16[1728,96]{1,0:T(8,128)(2,1)}, bf16[1728,96]{1,0:T(8,128)(2,1)S(1)}, u32[]{:S(2)}, u32[]{:S(2)}) collective-permute-start(bf16[1728,96]{1,0:T(8,128)(2,1)} %bitcast.15), channel_id=1, source_target_pairs={{0,1},{1,0},{2,3},{3,2},{4,5},{5,4},{6,7},{7,6},{8,9},{9,8},{10,11... | collective-permute-start | bytes 995336 | tf_op jit(solution)/shard_map/ppermute | solution.py:542
  1.2 24.6 %collective-permute-start.6 = (bf16[1728,96]{1,0:T(8,128)(2,1)}, bf16[1728,96]{1,0:T(8,128)(2,1)S(1)}, u32[]{:S(2)}, u32[]{:S(2)}) collective-permute-start(bf16[1728,96]{1,0:T(8,128)(2,1)} %bitcast.16), channel_id=1, source_target_pairs={{0,2},{1,3},{2,0},{3,1},{4,6},{5,7},{6,4},{7,5},{8,10},{9,11},{10,... | collective-permute-start | bytes 995336 | tf_op jit(solution)/shard_map/ppermute | solution.py:542
  5.6 7.6 %collective-permute-start = (bf16[2,3,64,96]{3,2,1,0:T(8,128)(2,1)S(1)}, bf16[2,3,64,96]{3,2,1,0:T(8,128)(2,1)S(1)}, u32[]{:S(2)}, u32[]{:S(2)}) collective-permute-start(bf16[2,3,64,96]{3,2,1,0:T(8,128)(2,1)S(1)} %broadcast_select_fusion.3), channel_id=1, source_target_pairs={{4,8},{12,0},{8,4},{0,12},{5,9},{13,1},{9,5},{1,13},{6,10},{14,2},... | collective-permute-start | bytes 221192 | tf_op jit(solution)/shard_map/ppermute | solution.py:456
  9.2 5.3 %collective-permute-start.1 = (bf16[2,3,64,96]{3,2,1,0:T(8,128)(2,1)S(1)}, bf16[2,3,64,96]{3,2,1,0:T(8,128)(2,1)S(1)}, u32[]{:S(2)}, u32[]{:S(2)}) collective-permute-start(bf16[2,3,64,96]{3,2,1,0:T(8,128)(2,1)S(1)} %get-tuple-element.44), channel_id=1, source_target_pairs={{0,4},{4,0},{8,12},{12,8},{1,5},{5,1},{9,13},{13,9},{2,6},{6,2},{1... | collective-permute-start | bytes 221192 | tf_op jit(solution)/shard_map/ppermute | solution.py:453
  17.3 6.9 %collective-permute-start.2 = (bf16[2,3,12,1216]{3,2,1,0:T(8,128)(2,1)}, bf16[2,3,12,1216]{3,2,1,0:T(8,128)(2,1)}, u32[]{:S(2)}, u32[]{:S(2)}) collective-permute-start(bf16[2,3,12,1216]{3,2,1,0:T(8,128)(2,1)} %get-tuple-element.47), channel_id=1, source_target_pairs={{1,2},{3,16},{17,18},{19,0},{2,1},{16,3},{18,17},{0,19},{5,6},{7,2... | collective-permute-start | bytes 525320 | tf_op jit(solution)/shard_map/ppermute | solution.py:456
  17.9 6.3 %collective-permute-start.3 = (bf16[2,3,12,1216]{3,2,1,0:T(8,128)(2,1)}, bf16[2,3,12,1216]{3,2,1,0:T(8,128)(2,1)}, u32[]{:S(2)}, u32[]{:S(2)}) collective-permute-start(bf16[2,3,12,1216]{3,2,1,0:T(8,128)(2,1)} %get-tuple-element.48), channel_id=1, source_target_pairs={{0,1},{1,0},{2,3},{3,2},{16,17},{17,16},{18,19},{19,18},{4,5},{5,4... | collective-permute-start | bytes 525320 | tf_op jit(solution)/shard_map/ppermute | solution.py:453
  17.9 5.9 %copy-start.12 = (f32[384]{0:T(512)S(1)}, f32[384]{0:T(512)}, u32[]{:S(2)}) copy-start(f32[384]{0:T(512)} %param.21) | copy-start | bytes 4612
  17.9 6.0 %copy-start.13 = (f32[384]{0:T(512)S(1)}, f32[384]{0:T(512)}, u32[]{:S(2)}) copy-start(f32[384]{0:T(512)} %param.24) | copy-start | bytes 4612
  25.4 1.7 %copy-start = (s32[3]{0:T(128)S(1)}, s32[3]{0:T(128)}, u32[]{:S(2)}) copy-start(s32[3]{0:T(128)} %pad_add_fusion.place.par) | copy-start | bytes 40
  25.4 1.7 %copy-start.4 = (f32[64]{0:T(128)S(1)}, f32[64]{0:T(128)}, u32[]{:S(2)}) copy-start(f32[64]{0:T(128)} %param.17) | copy-start | bytes 772
  25.4 1.7 %copy-start.9 = (f32[16,1024]{1,0:T(8,128)S(1)}, f32[16,1024]{1,0:T(8,128)}, u32[]{:S(2)}) copy-start(f32[16,1024]{1,0:T(8,128)} %get-tuple-element.24.masks) | copy-start | bytes 196612
  25.4 1.7 %copy-start.10 = (bf16[256,768]{1,0:T(8,128)(2,1)S(1)}, bf16[256,768]{1,0:T(8,128)(2,1)}, u32[]{:S(2)}) copy-start(bf16[256,768]{1,0:T(8,128)(2,1)} %get-tuple-element.23.w1) | copy-start | bytes 1179652
  25.8 10.2 %collective-permute-start.8 = (bf16[1728,96]{1,0:T(8,128)(2,1)S(1)}, bf16[1728,96]{1,0:T(8,128)(2,1)S(1)}, u32[]{:S(2)}, u32[]{:S(2)}) collective-permute-start(bf16[1728,96]{1,0:T(8,128)(2,1)S(1)} %collective-permute-done.6.refs_1_), channel_id=1, source_target_pairs={{0,1},{1,0},{2,3},{3,2},{4,5},{5,4},{6,7},{7,6},{8,9},{9,8},{10,11... | collective-permute-start | bytes 995336 | tf_op jit(solution)/shard_map/ppermute | solution.py:542
  27.1 8.9 %copy-start.1 = (bf16[3,3,192,96]{3,2,1,0:T(8,128)(2,1)S(1)}, bf16[3,3,192,96]{3,2,1,0:T(8,128)(2,1)}, u32[]{:S(2)}) copy-start(bf16[3,3,192,96]{3,2,1,0:T(8,128)(2,1)} %param.20) | copy-start | bytes 995332
  27.1 8.9 %copy-start.5 = (f32[64]{0:T(128)S(1)}, f32[64]{0:T(128)}, u32[]{:S(2)}) copy-start(f32[64]{0:T(128)} %param.22) | copy-start | bytes 772
  33.5 8.6 %collective-permute-start.4 = (bf16[512,256]{1,0:T(8,128)(2,1)S(1)}, bf16[512,256]{1,0:T(8,128)(2,1)S(1)}, u32[]{:S(2)}, u32[]{:S(2)}) collective-permute-start(bf16[512,256]{1,0:T(8,128)(2,1)S(1)} %get-tuple-element.26), channel_id=1, source_target_pairs={{0,1},{1,0},{2,3},{3,2},{16,17},{17,16},{18,19},{19,18},{4,5},{5,4... | collective-permute-start | bytes 786440 | tf_op jit(solution)/shard_map/ppermute | solution.py:453
  34.0 8.0 %collective-permute-start.5 = (bf16[512,256]{1,0:T(8,128)(2,1)S(1)}, bf16[512,256]{1,0:T(8,128)(2,1)S(1)}, u32[]{:S(2)}, u32[]{:S(2)}) collective-permute-start(bf16[512,256]{1,0:T(8,128)(2,1)S(1)} %get-tuple-element.27), channel_id=1, source_target_pairs={{1,2},{3,16},{17,18},{19,0},{2,1},{16,3},{18,17},{0,19},{5,6},{7,2... | collective-permute-start | bytes 786440 | tf_op jit(solution)/shard_map/ppermute | solution.py:456
  36.0 6.1 %copy-start.2 = (f32[192]{0:T(256)S(1)}, f32[192]{0:T(256)}, u32[]{:S(2)}) copy-start(f32[192]{0:T(256)} %param.19) | copy-start | bytes 2308
  36.0 6.1 %copy-start.3 = (f32[192]{0:T(256)S(1)}, f32[192]{0:T(256)}, u32[]{:S(2)}) copy-start(f32[192]{0:T(256)} %param.23) | copy-start | bytes 2308
  36.0 6.1 %copy-start.8 = (bf16[768,2304]{1,0:T(8,128)(2,1)S(1)}, bf16[768,2304]{1,0:T(8,128)(2,1)}, u32[]{:S(2)}) copy-start(bf16[768,2304]{1,0:T(8,128)(2,1)} %get-tuple-element.28.w2) | copy-start | bytes 10616836
  39.7 1.2 %copy-start.6 = (f32[2,2,256,384]{3,2,1,0:T(8,128)}, f32[2,2,256,384]{3,2,1,0:T(8,128)S(1)}, u32[]{:S(2)}) copy-start(f32[2,2,256,384]{3,2,1,0:T(8,128)S(1)} %get-tuple-element.39.base_in) | copy-start | bytes 4718596
  40.9 1.1 %copy-start.7 = (f32[2,2,256,384]{3,2,1,0:T(8,128)}, f32[2,2,256,384]{3,2,1,0:T(8,128)S(1)}, u32[]{:S(2)}) copy-start(f32[2,2,256,384]{3,2,1,0:T(8,128)S(1)} %get-tuple-element.40.gain_in) | copy-start | bytes 4718596
  61.2 0.8 %copy-start.11 = (bf16[768,384]{1,0:T(8,128)(2,1)}, bf16[768,384]{1,0:T(8,128)(2,1)S(1)}, u32[]{:S(2)}) copy-start(bf16[768,384]{1,0:T(8,128)(2,1)S(1)} %get-tuple-element.35.d2) | copy-start | bytes 1769476
  62.0 5.4 %collective-permute-start.9 = (bf16[384,256]{1,0:T(8,128)(2,1)S(1)}, bf16[384,256]{1,0:T(8,128)(2,1)S(1)}, u32[]{:S(2)}, u32[]{:S(2)}) collective-permute-start(bf16[384,256]{1,0:T(8,128)(2,1)S(1)} %get-tuple-element.36), channel_id=1, source_target_pairs={{0,1},{1,0},{2,3},{3,2},{16,17},{17,16},{18,19},{19,18},{4,5},{5,4... | collective-permute-start | bytes 589832 | tf_op jit(solution)/shard_map/ppermute | solution.py:453
  62.6 6.1 %collective-permute-start.10 = (bf16[384,256]{1,0:T(8,128)(2,1)S(1)}, bf16[384,256]{1,0:T(8,128)(2,1)S(1)}, u32[]{:S(2)}, u32[]{:S(2)}) collective-permute-start(bf16[384,256]{1,0:T(8,128)(2,1)S(1)} %get-tuple-element.37), channel_id=1, source_target_pairs={{1,2},{3,16},{17,18},{19,0},{2,1},{16,3},{18,17},{0,19},{5,6},{7,2... | collective-permute-start | bytes 589832 | tf_op jit(solution)/shard_map/ppermute | solution.py:456
  64.6 16.0 %all-to-all-start = ((f32[32,8,128]{2,1,0:T(8,128)}), f32[32,8,128]{2,1,0:T(8,128)S(1)}, u32[]{:S(2)}, u32[]{:S(2)}) async-start(f32[32,8,128]{2,1,0:T(8,128)} %get-tuple-element.34), calls=%async_computation | async-start | bytes 262144 | tf_op jit(solution)/shard_map/share/all_to_all | solution.py:611
  67.4 1.3 %copy-start.14 = (bf16[384,256]{1,0:T(8,128)(2,1)}, bf16[384,256]{1,0:T(8,128)(2,1)S(1)}, u32[]{:S(2)}) copy-start(bf16[384,256]{1,0:T(8,128)(2,1)S(1)} %collective-permute-done.9.rec_a) | copy-start | bytes 589828
  68.7 0.7 copy-start.15

commit v2 on v1

--- a/solution.py
+++ b/solution.py
@@ -7,6 +7,7 @@
 from jax.experimental import pallas as pl
 from jax.experimental.pallas import tpu as pltpu
 from jax.sharding import PartitionSpec as P
+
 
 OFFSETS = (-0.03, -0.088, -0.188)
 SPREADS = (0.458, 0.448, 0.45)
@@ -165,7 +166,9 @@
         copy.wait()
 
 
-def cells_kernel(R, C, par, img, w1, b1, masks, pre, pool, msg_a, msg_b, sel, z, p1):
+def cells_kernel(
+    R, C, par, both, left, right, over, under, w1, b1, masks, pre, pool, msg_a, msg_b, sel, img, z, p1
+):
     W = C + 2 * HJ
     G = W + 4
     frame = up128((R + 1) * W)
@@ -178,11 +181,18 @@
         n = lax.broadcasted_iota(jnp.int32, (K, tile), 1) + t * tile
         want = (p & (S - 1)) * G + (p >> 4)
         sel[:, t * tile : (t + 1) * tile] = jnp.where((n == want) & (p < px), 1.0, 0.0).astype(BF16)
+    above, below = over[...].astype(F32), under[...].astype(F32)
     for f in range(2):
-        for t in range(K // tile):
-            z[f, :, t * tile : (t + 1) * tile] = jnp.dot(
-                img[f], sel[:, t * tile : (t + 1) * tile], preferred_element_type=F32
-            )
+        for c in range(3):
+            r = (f * 3 + c) * RIM
+            mine = jnp.concatenate([v[f, c].astype(F32) for v in (left, both, right)], axis=1)
+            whole = jnp.concatenate([above[r : r + RIM], mine, below[r : r + RIM]], axis=0)
+            row = (f * 3 + c) * rows
+            img[row : row + rows, :] = jnp.concatenate([whole, jnp.zeros((rows, K - px), F32)], axis=1)
+    pixels = img[...].astype(BF16)
+    for t in range(K // tile):
+        lanes = slice(t * tile, (t + 1) * tile)
+        z[:, lanes] = jnp.dot(pixels, sel[:, lanes], preferred_element_type=F32)
     own = masks[0:1, 0 : R * W]
     bias = wide(column(b1, 4), tile)
     for pi in range(2):
@@ -197,7 +207,8 @@
                         r = top + S * k
                         parts.append(
                             jnp.concatenate(
-                                [z[f, c * rows + r : c * rows + r + S, lane : lane + W] for c in range(3)], axis=0
+                                [z[(f * 3 + c) * rows + r : (f * 3 + c) * rows + r + S, lane : lane + W] for c in range(3)],
+                                axis=0,
                             )
                         )
                     parts.append(jnp.zeros((3 * S, frame - (R + 1) * W), F32))
@@ -224,13 +235,9 @@
                 pool[row : row + quarter, :] = lanes_of(mine, 0, R * W, pool.shape[1]).astype(BF16)
 
 
-def first_grad_kernel(R, C, order, place, pre, lin, masks, b3, lin3, *refs):
-    k3, (base, gain, loss, w3, w3b, consts, bias) = refs[: len(order)], refs[len(order) :]
+def first_grad_kernel(pre, lin, masks, base, gain, loss):
     frame = base.shape[3]
     ch = lin.shape[1]
-    c2 = w3b.shape[0]
-    c3 = w3.shape[0]
-    shard = k3[0].shape[1]
     total = jnp.zeros((1, frame), F32)
     weights = wide(column(lin), frame)
     for pi in range(2):
@@ -243,6 +250,13 @@
                 gain[pi, pj, t * ch : (t + 1) * ch, :] = 0.25 * slope
                 total = total + jnp.where(masks[1 + pi : 2 + pi, 0:frame] > 0.0, part, 0.0)
     loss[...] = jnp.broadcast_to(total, loss.shape)
+
+
+def third_weights_kernel(order, place, b3, lin3, *refs):
+    k3, (w3, w3b, consts, bias) = refs[: len(order)], refs[len(order) :]
+    c2 = w3b.shape[0]
+    c3 = w3.shape[0]
+    shard = k3[0].shape[1]
     bias[0] = column(b3)
     bias[1] = column(lin3)
     for n, flip in enumerate(order):
@@ -391,12 +405,14 @@
             [jnp.zeros((64, GUARD), F32), whole, jnp.zeros((64, ext - GUARD - (R + 4) * W), F32)], axis=1
         ).astype(BF16)
     shift_all(p2b, 0, s4, 0, c2, window(W, 4), frame)
-    for copy in fetch:
-        copy.wait()
+    fetch[0].wait()
     for qi in range(2):
         around = p2b[(1 - qi) * 3 * c2 : (4 - qi) * 3 * c2, :]
         up = jnp.dot(w2b[qi * 2 * ch : (qi + 1) * 2 * ch, :], around, preferred_element_type=F32)
         good = masks[8 + qi : 9 + qi, 0:frame] > 0.0
+        if qi == 0:
+            fetch[1].wait()
+            fetch[2].wait()
         for qj in range(2):
             part = up[qj * ch : (qj + 1) * ch]
             for t in range(4):
@@ -406,6 +422,7 @@
                 s5[row : row + ch, 0:GUARD] = jnp.zeros((ch, GUARD), BF16)
                 s5[row : row + ch, GUARD : GUARD + frame] = jnp.where(good, d, 0.0).astype(BF16)
                 s5[row : row + ch, GUARD + frame :] = jnp.zeros((ch, s5.shape[1] - GUARD - frame), BF16)
+    fetch[3].wait()
     for qi in range(2):
         for qj in range(2):
             for wi in range(4):
@@ -456,11 +473,8 @@
     return first, lax.ppermute(b, axis, second)
 
 
-def neighbours(values, dim, width, axis, where, count):
+def neighbours(head, tail, axis, where, count):
     even = where % 2 == 0
-    size = values.shape[dim]
-    head = lax.slice_in_dim(values, 0, width, axis=dim)
-    tail = lax.slice_in_dim(values, size - width, size, axis=dim)
     a, b = swap(jnp.where(even, tail, head), jnp.where(even, head, tail), axis)
     zero = jnp.zeros_like(head)
     before = jnp.where(where > 0, jnp.where(even, b, a), zero)
@@ -490,7 +504,7 @@
         out_specs=out_specs,
         scratch_shapes=scratch,
         compiler_params=pltpu.CompilerParams(vmem_limit_bytes=limit * 2**20),
-        cost_estimate=pl.CostEstimate(flops=work * 10**9, bytes_accessed=2**20, transcendentals=0),
+        cost_estimate=pl.CostEstimate(flops=int(work * 10**9), bytes_accessed=2**20, transcendentals=0),
     )(*args)
 
 
@@ -533,26 +547,35 @@
         ],
         62, 5, place, want, kernel_one.reshape(-1, ch1), kernel_two, far=(2, 3),
     )
+    offsets = jnp.array(OFFSETS, F32)[:, None, None]
+    spreads = jnp.array(SPREADS, F32)[:, None, None]
+
+    def normed(cut):
+        return jnp.stack([((cut(image) - offsets) / spreads).astype(BF16) for image in (image_gen, image_ref)])
+
+    edge = HJ * S
+    left, right = neighbours(
+        normed(lambda image: image[:, :, :edge]), normed(lambda image: image[:, :, -edge:]), "col", at_col, across
+    )
+    both = normed(lambda image: image)
+
+    def strip(rows):
+        whole = jnp.concatenate([left[:, :, rows], both[:, :, rows], right[:, :, rows]], axis=3)
+        return whole.reshape(6 * RIM, W * S)
+
+    over, under = neighbours(strip(slice(0, RIM)), strip(slice(-RIM, None)), ROWS, at_row, high)
+    span = (W + 4) * S
+    over, under, kernel_three, w1, masks = lax.optimization_barrier((over, under, kernel_three, w1, masks))
     parts = lax.axis_size("chan")
-    pieces = [kernel_three.reshape(-1, shard)]
-    order = [0]
-    step = parts // 2
-    while step > 0:
+
+    def widen(pieces, order, step):
         pairs = [(i, i ^ step) for i in range(parts)]
         pieces = pieces + [lax.ppermute(piece, "chan", pairs) for piece in pieces]
-        order = order + [n ^ step for n in order]
-        step //= 2
-
-    offsets = jnp.array(OFFSETS, F32)[:, None, None]
-    spreads = jnp.array(SPREADS, F32)[:, None, None]
-    both = jnp.stack([((image - offsets) / spreads).astype(BF16) for image in (image_gen, image_ref)])
-    left, right = neighbours(both, 3, HJ * S, "col", at_col, across)
-    rim = jnp.concatenate([left, both, right], axis=3)
-    over, under = neighbours(rim, 2, RIM, ROWS, at_row, high)
-    rim = jnp.concatenate([over, rim, under], axis=2)
-    span = (W + 4) * S
-    rim = jnp.pad(rim, ((0, 0), (0, 0), (0, 0), (0, span - W * S)))
-    rim = rim.reshape(2, 3 * (R * S + 2 * RIM), span)
+        return pieces, order + [n ^ step for n in order]
+
+    pieces, order, step = [kernel_three.reshape(-1, shard)], [0], parts // 2
+    if step > 0:
+        pieces, order = widen(pieces, order, step)
 
     def flat(values):
         return values.reshape(1, -1)
@@ -572,16 +595,26 @@
             arr((8 * ch1, up128(3 * W)), BF16),
             arr((8 * ch1, up128(3 * W)), BF16),
         ),
-        [pltpu.VMEM((span, span), BF16), pltpu.VMEM((2, rows, span), F32), pltpu.VMEM((768, 2 * frame), BF16)],
-        18, 5, place, rim, w1, b1, masks,
+        [pltpu.VMEM((span, span), BF16), pltpu.VMEM((2 * rows, span), F32), pltpu.VMEM((2 * rows, span), F32),
+         pltpu.VMEM((768, 2 * frame), BF16)],
+        24, 5, place, both, left, right, over, under, w1, b1, masks,
     )
     rec_a, rec_b = swap(msg_a, msg_b, ROWS)
-    base, gain, loss1, w3, w3b, consts = call(
-        functools.partial(first_grad_kernel, R, C, tuple(order)),
-        (arr((2, 2, 4 * ch1, frame)), arr((2, 2, 4 * ch1, frame)), arr((8, frame)),
-            arr((ch3, 9 * ch2), BF16), arr((ch2, 9 * ch3), BF16), arr((2, ch3, 128))),
+    base, gain, loss1 = call(
+        first_grad_kernel,
+        (arr((2, 2, 4 * ch1, frame)), arr((2, 2, 4 * ch1, frame)), arr((8, frame))),
+        [],
+        12, 3, pre, lin1, masks,
+    )
+    loss1, pieces = lax.optimization_barrier((loss1, pieces))
+    while step > 1:
+        step //= 2
+        pieces, order = widen(pieces, order, step)
+    w3, w3b, consts = call(
+        functools.partial(third_weights_kernel, tuple(order)),
+        (arr((ch3, 9 * ch2), BF16), arr((ch2, 9 * ch3), BF16), arr((2, ch3, 128))),
         [pltpu.VMEM((2, ch3, 128), F32)],
-        12, 3, place, pre, lin1, masks, b3, lin3, *pieces,
+        12, 2, place, b3, lin3, *pieces,
     )
     ext1 = GUARD + up128((R + 6) * W) + GUARD
     everyone = high * across
@@ -607,8 +640,7 @@
         30, 10, place, pool, rec_a, rec_b, masks, w2, b2, lin2, w3, consts, w3b, loss1,
     )
     rec_a, rec_b = swap(msg_a, msg_b, ROWS)
-    with jax.named_scope("share"):
-        everywhere = lax.all_to_all(each, ("row", "col", "chan"), 0, 0)
+    everywhere = lax.all_to_all(each, ("row", "col", "chan"), 0, 0)
     image_grad = call(
         functools.partial(last_kernel, R, C),
         arr(image_gen.shape),

time: 82.4 us -> 83.3 us (1.011)
  waiting for transfers between devices: 5.42 us -> 9.31 us
  local copies, waits for them, and re-layouts: 5.8 us -> 2.98 us
  other arithmetic: 6.32 us -> 4.26 us
  starting transfers between devices: 16.6 us -> 17.7 us
    ppermute x4, starting transfers between devices: 1.22 us -> 6.31 us  [swap(): first = lax.ppermute(a, axis, [(i, i ^ 1) for i in range(count)])]
    ppermute x4, waiting for transfers between devices: 3.99 us -> 6.97 us  [swap(): return (first, lax.ppermute(b, axis, second))]
    ppermute x3, starting transfers between devices: 4.43 us -> 1.95 us  [widen(): pieces = pieces + [lax.ppermute(piece, 'chan', pairs) for piece in pieces]]
    ppermute x4, starting transfers between devices: 8.21 us -> 5.82 us  [swap(): return (first, lax.ppermute(b, axis, second))]
    ppermute x3, waiting for transfers between devices: 0.01 us -> 2.33 us  [widen(): pieces = pieces + [lax.ppermute(piece, 'chan', pairs) for piece in pieces]]
    unnamed x32 -> x34, local copies, waits for them, and re-layouts: 3.92 us -> 2.41 us
    concatenate x1 -> x2, local copies, waits for them, and re-layouts: 1.88 us -> 0.41 us  [strip(): jnp.concatenate([left[:, :, rows], both[:, :, rows], right[:, :, rows]],...]
    ppermute x4, waiting for transfers between devices: 1.42 us -> 0.01 us  [swap(): first = lax.ppermute(a, axis, [(i, i ^ 1) for i in range(count)])]
  transfers between devices with their start and end apart: 12 -> 12, of which waited for: 4 -> 5; matrix products, arithmetic and copies ran while one was open for 9% -> 3% of each run, Pallas kernels for 33% -> 34%
where the time goes in v2:
time: 83.3 us; the launch traced here: 82 us
  Pallas kernels  46.7 us (56%)
  starting transfers between devices  17.7 us (21%)
  waiting for transfers between devices  9.31 us (11%)
  other arithmetic  4.26 us (5%)
  local copies, waits for them, and re-layouts  2.98 us (4%)
  between operations  1.01 us (1%)
    pallas_call x6, Pallas kernels, call(): pl.pallas_call(kernel, out_shape=outs, in_specs=specs, out_specs=out_spec...  46.7 us
    ppermute x4, waiting for transfers between devices, swap(): return (first, lax.ppermute(b, axis, second))  6.97 us
    ppermute x4, starting transfers between devices, swap(): first = lax.ppermute(a, axis, [(i, i ^ 1) for i in range(count)])  6.31 us
    ppermute x4, starting transfers between devices, swap(): return (first, lax.ppermute(b, axis, second))  5.82 us
    all_to_all x1, starting transfers between devices, local(): everywhere = lax.all_to_all(each, ('row', 'col', 'chan'), 0, 0)  3.65 us
    another operation x4, other arithmetic, normed(): jnp.stack([((cut(image) - offsets) / spreads).astype(BF16) for image in (...  2.82 us
    unnamed x34, local copies, waits for them, and re-layouts  2.41 us
    ppermute x3, waiting for transfers between devices, widen(): pieces = pieces + [lax.ppermute(piece, 'chan', pairs) for piece in pieces]  2.33 us
  transfers between devices with their start and end apart: 12, of which 5 were waited for; matrix products, arithmetic and copies ran while one was open for 3% of the time, Pallas kernels for 34%

profile of v2, /device:TPU:0, one launch (start us, length us, event | category | flops | bytes accessed | tf_op | source)
XLA Modules:
  0.0 82.0 jit_solution(16837882193697993249)
XLA Ops:
  0.7 1.3 %fusion.4 = (bf16[1,3,64,96]{3,2,1,0:T(8,128)(2,1)S(1)}, bf16[1,3,64,96]{3,2,1,0:T(8,128)(2,1)S(1)}, bf16[1,3,64,96]{3,2,1,0:T(8,128)(2,1)S(1)}, bf16[1,3,64,96]{3,2,1,0:T(8,128)(2,1)S(1)}) fusion(f32[3,64,1024]{2,1,0:T(8,128)} %param.14, f32[3]{0:T(128)} %constant.51, f32[3]{0:T(128)} %constant.57, f32[3,64,1024]{2,1,0:T(8,128)} %param.15), kind=kLoop, calls=%fused_computation.25 | loop fusion | flops 221184 | bytes 442392 | tf_op jit(solution)/shard_map/stack | solution.py:554
  2.0 3.1 %collective-permute-start.1 = (bf16[2,3,64,96]{3,2,1,0:T(8,128)(2,1)S(1)}, bf16[2,3,64,96]{3,2,1,0:T(8,128)(2,1)S(1)}, u32[]{:S(2)}, u32[]{:S(2)}) collective-permute-start(bf16[2,3,64,96]{3,2,1,0:T(8,128)(2,1)S(1)} %get-tuple-element.72), channel_id=1, source_target_pairs={{0,4},{4,0},{8,12},{12,8},{1,5},{5,1},{9,13},{13,9},{2,6},{6,2},{1... | collective-permute-start | bytes 221192 | tf_op jit(solution)/shard_map/ppermute | solution.py:470
  5.1 2.5 %collective-permute-start = (bf16[2,3,64,96]{3,2,1,0:T(8,128)(2,1)S(1)}, bf16[2,3,64,96]{3,2,1,0:T(8,128)(2,1)S(1)}, u32[]{:S(2)}, u32[]{:S(2)}) collective-permute-start(bf16[2,3,64,96]{3,2,1,0:T(8,128)(2,1)S(1)} %get-tuple-element.73), channel_id=1, source_target_pairs={{4,8},{12,0},{8,4},{0,12},{5,9},{13,1},{9,5},{1,13},{6,10},{14,2},... | collective-permute-start | bytes 221192 | tf_op jit(solution)/shard_map/ppermute | solution.py:473
  7.6 1.4 %fusion = (bf16[1,3,64,1024]{3,2,1,0:T(8,128)(2,1)S(1)}, bf16[1,3,64,1024]{3,2,1,0:T(8,128)(2,1)S(1)}) fusion(f32[3,64,1024]{2,1,0:T(8,128)S(1)} %copy-done.12, f32[3]{0:T(128)} %constant.51, f32[3]{0:T(128)} %constant.57, f32[3,64,1024]{2,1,0:T(8,128)} %param.15), kind=kLoop, calls=%fused_computation.7 | loop fusion | flops 1179648 | bytes 2359320 | tf_op jit(solution)/shard_map/stack | solution.py:554
  9.1 0.7 pad_add_fusion.place.par
  9.8 2.5 %collective-permute-done = bf16[2,3,64,96]{3,2,1,0:T(8,128)(2,1)S(1)} collective-permute-done((bf16[2,3,64,96]{3,2,1,0:T(8,128)(2,1)S(1)}, bf16[2,3,64,96]{3,2,1,0:T(8,128)(2,1)S(1)}, u32[]{:S(2)}, u32[]{:S(2)}) %collective-permute-start) | collective-permute-done | bytes 73760 | tf_op jit(solution)/shard_map/ppermute | solution.py:473
  12.3 0.2 concatenate.7
  12.5 0.2 concatenate.6
  12.7 0.1 select_n.100
  12.9 0.8 collective-permute-start.2
  13.7 0.9 %collective-permute-start.3 = (bf16[72,1216]{1,0:T(8,128)(2,1)S(1)}, bf16[72,1216]{1,0:T(8,128)(2,1)S(1)}, u32[]{:S(2)}, u32[]{:S(2)}) collective-permute-start(bf16[72,1216]{1,0:T(8,128)(2,1)S(1)} %select_n.100), channel_id=1, source_target_pairs={{0,1},{1,0},{2,3},{3,2},{16,17},{17,16},{18,19},{19,18},{4,5},{5,4... | collective-permute-start | bytes 525320 | tf_op jit(solution)/shard_map/ppermute | solution.py:470
  14.6 5.9 %shard_map.149 = (bf16[256,768]{1,0:T(8,128)(2,1)}, bf16[192,1024]{1,0:T(8,128)(2,1)}, bf16[768,2304]{1,0:T(8,128)(2,1)}, bf16[256,6912]{1,0:T(8,128)(2,1)}, f32[16,1024]{1,0:T(8,128)}) custom-call(s32[3]{0:T(128)} %pad_add_fusion.place.par, s32[1,432]{1,0:T(1,128)} %constant.48.clone.want, bf16[432,64]{1,0:T(8,128)(2,1)} %bitcast.28, bf16[5,5,64,192]{3,2,1,0:T(8,128)(2,1)} %k2.1), custom_call_target="tpu_custom_call" | custom-call | flops 5000000000 | bytes 1048576 | tf_op jit(solution)/shard_map/pallas_call | solution.py:500
  20.6 0.1 pad_maximum_fusion.both
  20.7 0.8 copy-done.1
  21.5 1.4 %collective-permute-start.6 = (bf16[1728,96]{1,0:T(8,128)(2,1)S(1)}, bf16[1728,96]{1,0:T(8,128)(2,1)S(1)}, u32[]{:S(2)}, u32[]{:S(2)}) collective-permute-start(bf16[1728,96]{1,0:T(8,128)(2,1)S(1)} %bitcast.21), channel_id=1, source_target_pairs={{0,2},{1,3},{2,0},{3,1},{4,6},{5,7},{6,4},{7,5},{8,10},{9,11},{10,... | collective-permute-start | bytes 995336 | tf_op jit(solution)/shard_map/ppermute | solution.py:573
  23.0 6.4 %shard_map.150 = (f32[2,2,256,768]{3,2,1,0:T(8,128)S(1)}, bf16[512,384]{1,0:T(8,128)(2,1)S(1)}, bf16[512,256]{1,0:T(8,128)(2,1)S(1)}, bf16[512,256]{1,0:T(8,128)(2,1)S(1)}) custom-call(s32[3]{0:T(128)S(1)} %copy-done, bf16[2,3,64,1024]{3,2,1,0:T(8,128)(2,1)S(1)} %pad_maximum_fusion.both, bf16[2,3,64,96]{3,2,1,0:T(8,128)(2,1)S(1)} %get-tuple-element.71.left, ...), custom_call_target="tpu_custom_call" | custom-call | flops 5000000000 | bytes 1048576 | tf_op jit(solution)/shard_map/pallas_call | solution.py:500
  29.5 2.1 %shard_map.151 = (f32[2,2,256,384]{3,2,1,0:T(8,128)S(1)}, f32[2,2,256,384]{3,2,1,0:T(8,128)S(1)}, f32[8,384]{1,0:T(8,128)S(1)}) custom-call(f32[2,2,256,768]{3,2,1,0:T(8,128)S(1)} %get-tuple-element.41.pre, f32[1,64]{1,0:T(1,128)S(1)} %bitcast.27, f32[16,1024]{1,0:T(8,128)S(1)} %copy-done.10), custom_call_target="tpu_custom_call" | custom-call | flops 3000000000 | bytes 1048576 | tf_op jit(solution)/shard_map/pallas_call | solution.py:500
  31.6 2.0 %collective-permute-done.6.refs_1_ = bf16[1728,96]{1,0:T(8,128)(2,1)S(1)} collective-permute-done((bf16[1728,96]{1,0:T(8,128)(2,1)S(1)}, bf16[1728,96]{1,0:T(8,128)(2,1)S(1)}, u32[]{:S(2)}, u32[]{:S(2)}) %collective-permute-start.6) | collective-permute-done | bytes 331808 | tf_op jit(solution)/shard_map/ppermute | solution.py:573
  33.6 0.5 collective-permute-start.8
  34.1 1.5 %collective-permute-start.5 = (bf16[512,256]{1,0:T(8,128)(2,1)S(1)}, bf16[512,256]{1,0:T(8,128)(2,1)S(1)}, u32[]{:S(2)}, u32[]{:S(2)}) collective-permute-start(bf16[512,256]{1,0:T(8,128)(2,1)S(1)} %get-tuple-element.39), channel_id=1, source_target_pairs={{1,2},{3,16},{17,18},{19,0},{2,1},{16,3},{18,17},{0,19},{5,6},{7,2... | collective-permute-start | bytes 786440 | tf_op jit(solution)/shard_map/ppermute | solution.py:473
  35.7 0.3 collective-permute-done.8.refs_3_
  36.0 1.7 %shard_map.152 = (bf16[384,1728]{1,0:T(8,128)(2,1)S(1)}, bf16[192,3456]{1,0:T(8,128)(2,1)S(1)}, f32[2,384,128]{2,1,0:T(8,128)S(1)}) custom-call(s32[3]{0:T(128)S(1)} %copy-done, f32[1,384]{1,0:T(1,128)S(1)} %reshape.40.b3, f32[1,384]{1,0:T(1,128)S(1)} %reshape.41.lin3, bf16[1728,96]{1,0:T(8,128)(2,1)S(1)} %bitcast.23, ...), custom_call_target="tpu_custom_call" | custom-call | flops 2000000000 | bytes 1048576 | tf_op jit(solution)/shard_map/pallas_call | solution.py:500
  37.8 3.1 %collective-permute-done.5.rec_b = bf16[512,256]{1,0:T(8,128)(2,1)S(1)} collective-permute-done((bf16[512,256]{1,0:T(8,128)(2,1)S(1)}, bf16[512,256]{1,0:T(8,128)(2,1)S(1)}, u32[]{:S(2)}, u32[]{:S(2)}) %collective-permute-start.5) | collective-permute-done | bytes 262176 | tf_op jit(solution)/shard_map/ppermute | solution.py:473
  40.9 18.9 %shard_map.153 = (bf16[768,384]{1,0:T(8,128)(2,1)S(1)}, bf16[384,256]{1,0:T(8,128)(2,1)S(1)}, bf16[384,256]{1,0:T(8,128)(2,1)S(1)}, f32[32,8,128]{2,1,0:T(8,128)}) custom-call(s32[3]{0:T(128)S(1)} %copy-done, bf16[512,384]{1,0:T(8,128)(2,1)S(1)} %get-tuple-element.37.pool, bf16[512,256]{1,0:T(8,128)(2,1)S(1)} %collective-permute-done.4.rec_a, ...), custom_call_target="tpu_custom_call" | custom-call | flops 10000000000 | bytes 1048576 | tf_op jit(solution)/shard_map/pallas_call | solution.py:500
  59.9 0.8 %copy-done.11 = bf16[768,384]{1,0:T(8,128)(2,1)} copy-done((bf16[768,384]{1,0:T(8,128)(2,1)}, bf16[768,384]{1,0:T(8,128)(2,1)S(1)}, u32[]{:S(2)}) %copy-start.11) | copy-done | bytes 589848
  60.7 2.3 %collective-permute-start.9 = (bf16[384,256]{1,0:T(8,128)(2,1)S(1)}, bf16[384,256]{1,0:T(8,128)(2,1)S(1)}, u32[]{:S(2)}, u32[]{:S(2)}) collective-permute-start(bf16[384,256]{1,0:T(8,128)(2,1)S(1)} %get-tuple-element.52), channel_id=1, source_target_pairs={{0,1},{1,0},{2,3},{3,2},{16,17},{17,16},{18,19},{19,18},{4,5},{5,4... | collective-permute-start | bytes 589832 | tf_op jit(solution)/shard_map/ppermute | solution.py:470
  63.0 1.0 %collective-permute-start.10 = (bf16[384,256]{1,0:T(8,128)(2,1)S(1)}, bf16[384,256]{1,0:T(8,128)(2,1)S(1)}, u32[]{:S(2)}, u32[]{:S(2)}) collective-permute-start(bf16[384,256]{1,0:T(8,128)(2,1)S(1)} %get-tuple-element.53), channel_id=1, source_target_pairs={{1,2},{3,16},{17,18},{19,0},{2,1},{16,3},{18,17},{0,19},{5,6},{7,2... | collective-permute-start | bytes 589832 | tf_op jit(solution)/shard_map/ppermute | solution.py:473
  64.0 3.6 %all-to-all-start = ((f32[32,8,128]{2,1,0:T(8,128)}), f32[32,8,128]{2,1,0:T(8,128)S(1)}, u32[]{:S(2)}, u32[]{:S(2)}) async-start(f32[32,8,128]{2,1,0:T(8,128)} %get-tuple-element.50), calls=%async_computation | async-start | bytes 262144 | tf_op jit(solution)/shard_map/all_to_all | solution.py:643
  67.7 1.4 %collective-permute-done.10.rec_b = bf16[384,256]{1,0:T(8,128)(2,1)S(1)} collective-permute-done((bf16[384,256]{1,0:T(8,128)(2,1)S(1)}, bf16[384,256]{1,0:T(8,128)(2,1)S(1)}, u32[]{:S(2)}, u32[]{:S(2)}) %collective-permute-start.10) | collective-permute-done | bytes 196640 | tf_op jit(solution)/shard_map/ppermute | solution.py:473
  69.1 0.7 copy-done.16
  69.8 11.6 %shard_map.154 = f32[3,64,1024]{2,1,0:T(8,128)} custom-call(s32[3]{0:T(128)} %pad_add_fusion.place.par, bf16[768,384]{1,0:T(8,128)(2,1)} %copy-done.11, bf16[384,256]{1,0:T(8,128)(2,1)} %copy-done.15, bf16[384,256]{1,0:T(8,128)(2,1)} %copy-done.16, f32[16,1024]{1,0:T(8,128)} %get-tuple-element.36.masks, bf16[256,6912]{1,0:T(8,128)(2,1)} %get-tuple-element.54.w2b_in, ...), custom_call_target="tpu_custom_call" | custom-call | flops 10000000000 | bytes 1048576 | tf_op jit(solution)/shard_map/pallas_call | solution.py:500
  81.4 0.6 slice_reduce_fusion
  (49 shorter events, 0.4 us)
Async XLA Ops:
  0.6 7.0 %copy-start.12 = (f32[3,64,1024]{2,1,0:T(8,128)S(1)}, f32[3,64,1024]{2,1,0:T(8,128)}, u32[]{:S(2)}) copy-start(f32[3,64,1024]{2,1,0:T(8,128)} %param.14) | copy-start | bytes 2359300
  2.0 7.8 %collective-permute-start.1 = (bf16[2,3,64,96]{3,2,1,0:T(8,128)(2,1)S(1)}, bf16[2,3,64,96]{3,2,1,0:T(8,128)(2,1)S(1)}, u32[]{:S(2)}, u32[]{:S(2)}) collective-permute-start(bf16[2,3,64,96]{3,2,1,0:T(8,128)(2,1)S(1)} %get-tuple-element.72), channel_id=1, source_target_pairs={{0,4},{4,0},{8,12},{12,8},{1,5},{5,1},{9,13},{13,9},{2,6},{6,2},{1... | collective-permute-start | bytes 221192 | tf_op jit(solution)/shard_map/ppermute | solution.py:470
  5.1 7.1 %collective-permute-start = (bf16[2,3,64,96]{3,2,1,0:T(8,128)(2,1)S(1)}, bf16[2,3,64,96]{3,2,1,0:T(8,128)(2,1)S(1)}, u32[]{:S(2)}, u32[]{:S(2)}) collective-permute-start(bf16[2,3,64,96]{3,2,1,0:T(8,128)(2,1)S(1)} %get-tuple-element.73), channel_id=1, source_target_pairs={{4,8},{12,0},{8,4},{0,12},{5,9},{13,1},{9,5},{1,13},{6,10},{14,2},... | collective-permute-start | bytes 221192 | tf_op jit(solution)/shard_map/ppermute | solution.py:473
  12.9 7.8 %collective-permute-start.2 = (bf16[72,1216]{1,0:T(8,128)(2,1)S(1)}, bf16[72,1216]{1,0:T(8,128)(2,1)S(1)}, u32[]{:S(2)}, u32[]{:S(2)}) collective-permute-start(bf16[72,1216]{1,0:T(8,128)(2,1)S(1)} %select_n.98), channel_id=1, source_target_pairs={{1,2},{3,16},{17,18},{19,0},{2,1},{16,3},{18,17},{0,19},{5,6},{7,2... | collective-permute-start | bytes 525320 | tf_op jit(solution)/shard_map/ppermute | solution.py:473
  13.7 7.0 %collective-permute-start.3 = (bf16[72,1216]{1,0:T(8,128)(2,1)S(1)}, bf16[72,1216]{1,0:T(8,128)(2,1)S(1)}, u32[]{:S(2)}, u32[]{:S(2)}) collective-permute-start(bf16[72,1216]{1,0:T(8,128)(2,1)S(1)} %select_n.100), channel_id=1, source_target_pairs={{0,1},{1,0},{2,3},{3,2},{16,17},{17,16},{18,19},{19,18},{4,5},{5,4... | collective-permute-start | bytes 525320 | tf_op jit(solution)/shard_map/ppermute | solution.py:470
  20.5 1.0 %copy-start.1 = (bf16[3,3,192,96]{3,2,1,0:T(8,128)(2,1)S(1)}, bf16[3,3,192,96]{3,2,1,0:T(8,128)(2,1)}, u32[]{:S(2)}) copy-start(bf16[3,3,192,96]{3,2,1,0:T(8,128)(2,1)} %param.20) | copy-start | bytes 995332
  20.5 2.4 %copy-start = (s32[3]{0:T(128)S(1)}, s32[3]{0:T(128)}, u32[]{:S(2)}) copy-start(s32[3]{0:T(128)} %pad_add_fusion.place.par) | copy-start | bytes 40
  20.5 2.4 %copy-start.4 = (f32[64]{0:T(128)S(1)}, f32[64]{0:T(128)}, u32[]{:S(2)}) copy-start(f32[64]{0:T(128)} %param.17) | copy-start | bytes 772
  20.5 2.4 %copy-start.9 = (bf16[256,768]{1,0:T(8,128)(2,1)S(1)}, bf16[256,768]{1,0:T(8,128)(2,1)}, u32[]{:S(2)}) copy-start(bf16[256,768]{1,0:T(8,128)(2,1)} %get-tuple-element.35.w1) | copy-start | bytes 1179652
  20.6 2.4 %copy-start.10 = (f32[16,1024]{1,0:T(8,128)S(1)}, f32[16,1024]{1,0:T(8,128)}, u32[]{:S(2)}) copy-start(f32[16,1024]{1,0:T(8,128)} %get-tuple-element.36.masks) | copy-start | bytes 196612
  21.5 12.1 %collective-permute-start.6 = (bf16[1728,96]{1,0:T(8,128)(2,1)S(1)}, bf16[1728,96]{1,0:T(8,128)(2,1)S(1)}, u32[]{:S(2)}, u32[]{:S(2)}) collective-permute-start(bf16[1728,96]{1,0:T(8,128)(2,1)S(1)} %bitcast.21), channel_id=1, source_target_pairs={{0,2},{1,3},{2,0},{3,1},{4,6},{5,7},{6,4},{7,5},{8,10},{9,11},{10,... | collective-permute-start | bytes 995336 | tf_op jit(solution)/shard_map/ppermute | solution.py:573
  23.0 6.4 %copy-start.5 = (f32[64]{0:T(128)S(1)}, f32[64]{0:T(128)}, u32[]{:S(2)}) copy-start(f32[64]{0:T(128)} %param.22) | copy-start | bytes 772
  29.4 6.2 %copy-start.13 = (f32[384]{0:T(512)S(1)}, f32[384]{0:T(512)}, u32[]{:S(2)}) copy-start(f32[384]{0:T(512)} %param.21) | copy-start | bytes 4612
  29.4 6.2 %copy-start.14 = (f32[384]{0:T(512)S(1)}, f32[384]{0:T(512)}, u32[]{:S(2)}) copy-start(f32[384]{0:T(512)} %param.24) | copy-start | bytes 4612
  31.6 6.2 %copy-start.6 = (f32[2,2,256,384]{3,2,1,0:T(8,128)}, f32[2,2,256,384]{3,2,1,0:T(8,128)S(1)}, u32[]{:S(2)}) copy-start(f32[2,2,256,384]{3,2,1,0:T(8,128)S(1)} %get-tuple-element.55.base_in) | copy-start | bytes 4718596
  31.6 6.2 %copy-start.7 = (f32[2,2,256,384]{3,2,1,0:T(8,128)}, f32[2,2,256,384]{3,2,1,0:T(8,128)S(1)}, u32[]{:S(2)}) copy-start(f32[2,2,256,384]{3,2,1,0:T(8,128)S(1)} %get-tuple-element.56.gain_in) | copy-start | bytes 4718596
  33.6 2.1 %collective-permute-start.7 = (bf16[1728,96]{1,0:T(8,128)(2,1)S(1)}, bf16[1728,96]{1,0:T(8,128)(2,1)S(1)}, u32[]{:S(2)}, u32[]{:S(2)}) collective-permute-start(bf16[1728,96]{1,0:T(8,128)(2,1)S(1)} %bitcast.22), channel_id=1, source_target_pairs={{0,1},{1,0},{2,3},{3,2},{4,5},{5,4},{6,7},{7,6},{8,9},{9,8},{10,11... | collective-permute-start | bytes 995336 | tf_op jit(solution)/shard_map/ppermute | solution.py:573
  33.6 2.4 %collective-permute-start.8 = (bf16[1728,96]{1,0:T(8,128)(2,1)S(1)}, bf16[1728,96]{1,0:T(8,128)(2,1)S(1)}, u32[]{:S(2)}, u32[]{:S(2)}) collective-permute-start(bf16[1728,96]{1,0:T(8,128)(2,1)S(1)} %collective-permute-done.6.refs_1_), channel_id=1, source_target_pairs={{0,1},{1,0},{2,3},{3,2},{4,5},{5,4},{6,7},{7,6},{8,9},{9,8},{10,11... | collective-permute-start | bytes 995336 | tf_op jit(solution)/shard_map/ppermute | solution.py:573
  34.1 3.7 %collective-permute-start.4 = (bf16[512,256]{1,0:T(8,128)(2,1)S(1)}, bf16[512,256]{1,0:T(8,128)(2,1)S(1)}, u32[]{:S(2)}, u32[]{:S(2)}) collective-permute-start(bf16[512,256]{1,0:T(8,128)(2,1)S(1)} %get-tuple-element.38), channel_id=1, source_target_pairs={{0,1},{1,0},{2,3},{3,2},{16,17},{17,16},{18,19},{19,18},{4,5},{5,4... | collective-permute-start | bytes 786440 | tf_op jit(solution)/shard_map/ppermute | solution.py:470
  34.1 6.8 %collective-permute-start.5 = (bf16[512,256]{1,0:T(8,128)(2,1)S(1)}, bf16[512,256]{1,0:T(8,128)(2,1)S(1)}, u32[]{:S(2)}, u32[]{:S(2)}) collective-permute-start(bf16[512,256]{1,0:T(8,128)(2,1)S(1)} %get-tuple-element.39), channel_id=1, source_target_pairs={{1,2},{3,16},{17,18},{19,0},{2,1},{16,3},{18,17},{0,19},{5,6},{7,2... | collective-permute-start | bytes 786440 | tf_op jit(solution)/shard_map/ppermute | solution.py:473
  35.6 5.3 %copy-start.2 = (f32[192]{0:T(256)S(1)}, f32[192]{0:T(256)}, u32[]{:S(2)}) copy-start(f32[192]{0:T(256)} %param.19) | copy-start | bytes 2308
  35.7 5.3 %copy-start.3 = (f32[192]{0:T(256)S(1)}, f32[192]{0:T(256)}, u32[]{:S(2)}) copy-start(f32[192]{0:T(256)} %param.23) | copy-start | bytes 2308
  35.7 5.2 %copy-start.8 = (bf16[768,2304]{1,0:T(8,128)(2,1)S(1)}, bf16[768,2304]{1,0:T(8,128)(2,1)}, u32[]{:S(2)}) copy-start(bf16[768,2304]{1,0:T(8,128)(2,1)} %get-tuple-element.40.w2) | copy-start | bytes 10616836
  59.9 0.8 %copy-start.11 = (bf16[768,384]{1,0:T(8,128)(2,1)}, bf16[768,384]{1,0:T(8,128)(2,1)S(1)}, u32[]{:S(2)}) copy-start(bf16[768,384]{1,0:T(8,128)(2,1)S(1)} %get-tuple-element.51.d2) | copy-start | bytes 1769476
  60.7 7.0 %collective-permute-start.9 = (bf16[384,256]{1,0:T(8,128)(2,1)S(1)}, bf16[384,256]{1,0:T(8,128)(2,1)S(1)}, u32[]{:S(2)}, u32[]{:S(2)}) collective-permute-start(bf16[384,256]{1,0:T(8,128)(2,1)S(1)} %get-tuple-element.52), channel_id=1, source_target_pairs={{0,1},{1,0},{2,3},{3,2},{16,17},{17,16},{18,19},{19,18},{4,5},{5,4... | collective-permute-start | bytes 589832 | tf_op jit(solution)/shard_map/ppermute | solution.py:470
  63.0 6.1 %collective-permute-start.10 = (bf16[384,256]{1,0:T(8,128)(2,1)S(1)}, bf16[384,256]{1,0:T(8,128)(2,1)S(1)}, u32[]{:S(2)}, u32[]{:S(2)}) collective-permute-start(bf16[384,256]{1,0:T(8,128)(2,1)S(1)} %get-tuple-element.53), channel_id=1, source_target_pairs={{1,2},{3,16},{17,18},{19,0},{2,1},{16,3},{18,17},{0,19},{5,6},{7,2... | collective-permute-start | bytes 589832 | tf_op jit(solution)/shard_map/ppermute | solution.py:473
  64.0 17.4 %all-to-all-start = ((f32[32,8,128]{2,1,0:T(8,128)}), f32[32,8,128]{2,1,0:T(8,128)S(1)}, u32[]{:S(2)}, u32[]{:S(2)}) async-start(f32[32,8,128]{2,1,0:T(8,128)} %get-tuple-element.50), calls=%async_computation | async-start | bytes 262144 | tf_op jit(solution)/shard_map/all_to_all | solution.py:643
  67.7 1.4 %copy-start.15 = (bf16[384,256]{1,0:T(8,128)(2,1)}, bf16[384,256]{1,0:T(8,128)(2,1)S(1)}, u32[]{:S(2)}) copy-start(bf16[384,256]{1,0:T(8,128)(2,1)S(1)} %collective-permute-done.9.rec_a) | copy-start | bytes 589828
  69.1 0.7 copy-start.16
